TPU v7x, 32 devices: a whole 2x2x4 slice. The times are simulated.
32 devices in a mesh: gx: 2 (over x), gy: 4 (over z), gz: 4 (over y, core).
Axes of the slice: x: 2, y: 2, z: 4, core: 2. Of those that a mesh axis runs over, the one named last changes fastest.
Arguments:
- fields: float32 [4, 8, 256, 512], P(None, 'gx', 'gy', 'gz'), may hold values from -8 to 8
- volume_code: int32 [8, 256, 512], P('gx', 'gy', 'gz'), may hold values from 65536 to 1048576
- cut_flag: int32 [8, 256, 512], P('gx', 'gy', 'gz'), may hold values 0 or 1
- member_bits: int32 [8, 256, 512], P('gx', 'gy', 'gz'), may hold values from 0 to 134217727
Outputs:
- merged: float32 [4, 8, 256, 512], P(None, 'gx', 'gy', 'gz')
All inputs are finite; a program needn't handle non-finite values. No bound on the sum of `cut_flag` on one device may be relied on, other than what follows from the above.
Results may differ from a plain program's by a relative error of at most 0.00015.
Values sent between devices are 32-bit elements; how exact they have to be, the bound alone decides.
No kernel may reach another device: no remote copies, remote signals or barrier semaphores. Data moves between devices by JAX's collectives and lax.ppermute only.
A program may use at most 128 MiB of HBM per device.

v0:
```python
import jax
import jax.numpy as jnp
from jax import lax
from jax.sharding import PartitionSpec as P

PASSES = 2


def extended(block, sides, width):
    for axis, dim in sides:
        count = lax.axis_size(axis)
        forward = [(i, i + 1) for i in range(count - 1)]
        forward.append((count - 1, 0))
        backward = [(target, source) for source, target in forward]
        low = lax.ppermute(
            lax.slice_in_dim(block, block.shape[dim] - width, None, axis=dim), axis, forward
        )
        high = lax.ppermute(lax.slice_in_dim(block, 0, width, axis=dim), axis, backward)
        block = jnp.concatenate([low, block, high], axis=dim)
    return block


def offset_list():
    result = []
    for dx in (-1, 0, 1):
        for dy in (-1, 0, 1):
            for dz in (-1, 0, 1):
                result.append((dx, dy, dz))
    return result


def member_bit(active, index):
    return jnp.bitwise_and(jnp.right_shift(active, index), 1).astype(jnp.float32)


def pulled_sums(padded, offsets, sizex, sizey, sizez):
    sums = jnp.zeros((5, sizex, sizey, sizez), jnp.float32)
    for index, shift in enumerate(offsets):
        dx, dy, dz = shift
        piece = padded[:, 1 - dx : 1 - dx + sizex, 1 - dy : 1 - dy + sizey, 1 - dz : 1 - dz + sizez]
        if index == 13:
            sums = sums + piece[:5]
        else:
            if index < 14:
                member = member_bit(piece[5].astype(jnp.int32), index)
            else:
                member = member_bit(piece[6].astype(jnp.int32), index - 14)
            sums = sums + member[None] * piece[:5]
    return sums


def body(fields, volume_code, cut_flag, member_bits):
    sizex, sizey, sizez = volume_code.shape
    kappa = volume_code.astype(jnp.float32) / 1048576.0
    active = member_bits * cut_flag
    offsets = offset_list()
    own_bits = []
    count = jnp.zeros_like(kappa)
    for index in range(27):
        if index == 13:
            member = jnp.ones_like(kappa)
        else:
            member = member_bit(active, index)
        own_bits.append(member)
        count = count + member
    low_part = jnp.bitwise_and(active, 16383).astype(jnp.float32)
    high_part = jnp.right_shift(active, 14).astype(jnp.float32)
    state = fields
    for step in range(PASSES):
        weighted = kappa[None] * state
        packed = jnp.concatenate([kappa[None], weighted, low_part[None], high_part[None]], axis=0)
        padded = extended(packed, (("gx", 1), ("gy", 2), ("gz", 3)), 1)
        sums = pulled_sums(padded, offsets, sizex, sizey, sizez)
        hat = sums[1:] / sums[0:1]
        framed = extended(hat, (("gx", 1), ("gy", 2), ("gz", 3)), 1)
        total = jnp.zeros_like(state)
        for index, shift in enumerate(offsets):
            dx, dy, dz = shift
            piece = framed[
                :, 1 + dx : 1 + dx + sizex, 1 + dy : 1 + dy + sizey, 1 + dz : 1 + dz + sizez
            ]
            total = total + own_bits[index][None] * piece
        state = total / count[None]
    return state


def solution(mesh):
    in_specs = (
        P(None, "gx", "gy", "gz"),
        P("gx", "gy", "gz"),
        P("gx", "gy", "gz"),
        P("gx", "gy", "gz"),
    )
    out_specs = P(None, "gx", "gy", "gz")
    return jax.shard_map(body, mesh=mesh, in_specs=in_specs, out_specs=out_specs, check_vma=False)
```

profile of v0, /device:TPU:0, one launch (start us, length us, event | category | flops | bytes accessed | tf_op | source)
XLA Modules:
  0.0 150.6 jit_solution(13559110110422947061)
XLA Ops:
  4.6 3.0 %collective-permute-start = (f32[7,1,64,128]{3,2,1,0:T(8,128)S(1)}, f32[7,1,64,128]{3,2,1,0:T(8,128)S(1)}, u32[]{:S(2)}, u32[]{:S(2)}) collective-permute-start(f32[7,1,64,128]{3,2,1,0:T(8,128)S(1)} %get-tuple-element.77), channel_id=1, source_target_pairs={{0,16},{16,0},{1,17},{17,1},{2,18},{18,2},{3,19},{19,3},{4,20},{20... | collective-permute-start | bytes 688136 | tf_op jit(solution)/shard_map/ppermute | solution.py:15
  7.7 6.4 %collective-permute-done = f32[7,1,64,128]{3,2,1,0:T(8,128)S(1)} collective-permute-done((f32[7,1,64,128]{3,2,1,0:T(8,128)S(1)}, f32[7,1,64,128]{3,2,1,0:T(8,128)S(1)}, u32[]{:S(2)}, u32[]{:S(2)}) %collective-permute-start) | collective-permute-done | bytes 229408 | tf_op jit(solution)/shard_map/ppermute | solution.py:15
  14.1 4.1 %collective-permute-done.1 = f32[7,1,64,128]{3,2,1,0:T(8,128)S(1)} collective-permute-done((f32[7,1,64,128]{3,2,1,0:T(8,128)S(1)}, f32[7,1,64,128]{3,2,1,0:T(8,128)S(1)}, u32[]{:S(2)}, u32[]{:S(2)}) %collective-permute-start.1) | collective-permute-done | bytes 229408 | tf_op jit(solution)/shard_map/ppermute | solution.py:18
  18.3 3.9 %collective-permute-start.3 = (f32[7,6,1,128]{3,0,2,1:T(8,128)S(1)}, f32[7,6,1,128]{3,0,2,1:T(8,128)S(1)}, u32[]{:S(2)}, u32[]{:S(2)}) collective-permute-start(f32[7,6,1,128]{3,0,2,1:T(8,128)S(1)} %copy.335), channel_id=1, source_target_pairs={{4,0},{8,4},{12,8},{0,12},{5,1},{9,5},{13,9},{1,13},{6,2},{10,6},{... | collective-permute-start | bytes 64520 | tf_op jit(solution)/shard_map/ppermute | solution.py:18
  23.7 4.1 %collective-permute-done.2 = f32[7,6,1,128]{3,0,2,1:T(8,128)S(1)} collective-permute-done((f32[7,6,1,128]{3,0,2,1:T(8,128)S(1)}, f32[7,6,1,128]{3,0,2,1:T(8,128)S(1)}, u32[]{:S(2)}, u32[]{:S(2)}) %collective-permute-start.2) | collective-permute-done | bytes 21536 | tf_op jit(solution)/shard_map/ppermute | solution.py:15
  29.7 2.6 %copy.298 = f32[7,6,66,1]{2,0,3,1:T(8,128)} copy(f32[7,6,66,1]{3,2,1,0:T(8,128)} %get-tuple-element.57) | data formatting | bytes 22176 | tf_op jit(solution)/shard_map/slice | solution.py:18
  37.0 2.5 %copy.299 = f32[7,6,66,1]{3,2,1,0:T(8,128)} copy(f32[7,6,66,1]{2,0,3,1:T(8,128)} %collective-permute-done.4) | data formatting | bytes 22176 | tf_op jit(solution)/shard_map/ppermute | solution.py:18
  39.5 1.8 %copy.302 = f32[7,6,66,1]{3,2,1,0:T(8,128)} copy(f32[7,6,66,1]{2,0,3,1:T(8,128)S(1)} %collective-permute-done.5) | data formatting | bytes 22176 | tf_op jit(solution)/shard_map/ppermute | solution.py:15
  41.2 6.1 %fusion.14 = (f32[7,6,66,129]{3,2,1,0:T(8,128)S(1)}, f32[7,6,66,129]{3,2,1,0:T(8,128)S(1)}) fusion(f32[1,4,64,128]{3,2,1,0:T(8,128)S(1)} %get-tuple-element.124, f32[1,4,64,128]{3,2,1,0:T(8,128)S(1)} %get-tuple-element.125, f32[1,4,64,128]{3,2,1,0:T(8,128)S(1)} %get-tuple-element.127, f32[7,6,66,1]{3,2,1,0:T(8,128)} %copy.299, ...), kind=kLoop, calls=%fused_computation.26 | loop fusion | flops 5721408 | bytes 4302144 | tf_op jit(solution)/shard_map/concatenate | solution.py:19
  49.6 2.9 %fusion.61 = f32[5,4,64,128]{3,2,1,0:T(8,128)S(1)} fusion(f32[1,4,64,128]{3,2,1,0:T(8,128)S(1)} %get-tuple-element.127, f32[7,6,66,129]{3,2,1,0:T(8,128)S(1)} %get-tuple-element.62, f32[7,6,65,128]{3,2,1,0:T(8,128)S(1)} %copy-done.3, f32[7,6,66,129]{3,2,1,0:T(8,128)S(1)} %get-tuple-element.61, f32[7,5,64,128]{3,2,1,0:T(8,128)S(1)} %copy-done.11, ...), kind=kLoop, calls=%fused_computation.127 | loop fusion | flops 8683520 | bytes 21757952 | tf_op jit(solution)/shard_map/add | solution.py:48
  54.7 4.1 %collective-permute-done.6 = f32[4,1,64,128]{3,2,1,0:T(8,128)S(1)} collective-permute-done((f32[4,1,64,128]{3,2,1,0:T(8,128)S(1)}, f32[4,1,64,128]{3,2,1,0:T(8,128)S(1)}, u32[]{:S(2)}, u32[]{:S(2)}) %collective-permute-start.6) | collective-permute-done | bytes 131104 | tf_op jit(solution)/shard_map/ppermute | solution.py:15
  58.9 2.8 %collective-permute-done.7 = f32[4,1,64,128]{3,2,1,0:T(8,128)S(1)} collective-permute-done((f32[4,1,64,128]{3,2,1,0:T(8,128)S(1)}, f32[4,1,64,128]{3,2,1,0:T(8,128)S(1)}, u32[]{:S(2)}, u32[]{:S(2)}) %collective-permute-start.7) | collective-permute-done | bytes 131104 | tf_op jit(solution)/shard_map/ppermute | solution.py:18
  61.8 2.0 %collective-permute-start.8 = (f32[4,6,1,128]{3,1,2,0:T(8,128)S(1)}, f32[4,6,1,128]{3,1,2,0:T(8,128)S(1)}, u32[]{:S(2)}, u32[]{:S(2)}) collective-permute-start(f32[4,6,1,128]{3,1,2,0:T(8,128)S(1)} %copy.304), channel_id=1, source_target_pairs={{0,4},{4,8},{8,12},{12,0},{1,5},{5,9},{9,13},{13,1},{2,6},{6,10},{... | collective-permute-start | bytes 36872 | tf_op jit(solution)/shard_map/ppermute | solution.py:15
  65.5 1.8 %collective-permute-done.8 = f32[4,6,1,128]{3,1,2,0:T(8,128)S(1)} collective-permute-done((f32[4,6,1,128]{3,1,2,0:T(8,128)S(1)}, f32[4,6,1,128]{3,1,2,0:T(8,128)S(1)}, u32[]{:S(2)}, u32[]{:S(2)}) %collective-permute-start.8) | collective-permute-done | bytes 12320 | tf_op jit(solution)/shard_map/ppermute | solution.py:15
  69.3 2.8 %collective-permute-done.10 = f32[4,6,66,1]{2,1,3,0:T(8,128)S(1)} collective-permute-done((f32[4,6,66,1]{2,1,3,0:T(8,128)S(1)}, f32[4,6,66,1]{2,1,3,0:T(8,128)S(1)}, u32[]{:S(2)}, u32[]{:S(2)}) %collective-permute-start.10) | collective-permute-done | bytes 6368 | tf_op jit(solution)/shard_map/ppermute | solution.py:15
  74.9 2.4 %maximum_maximum_fusion = (f32[4,6,66,129]{3,2,1,0:T(8,128)S(1)}, f32[4,6,66,129]{3,2,1,0:T(8,128)S(1)}) fusion(f32[4,6,1,128]{3,2,1,0:T(1,128)S(1)} %copy.307, f32[4,1,64,128]{3,2,1,0:T(8,128)S(1)} %collective-permute-done.7, f32[4,4,64,128]{3,2,1,0:T(8,128)S(1)} %slice_divide_fusion.1, f32[4,1,64,128]{3,2,1,0:T(8,128)S(1)} %collective-permute-done.6, ...), kind=kLoop, calls=%fused_computation.56 | loop fusion | flops 2043360 | bytes 2458368 | tf_op jit(solution)/shard_map/concatenate | solution.py:19
  77.6 2.6 %fusion.131 = f32[4,4,64,128]{3,2,1,0:T(8,128)S(1)} fusion(f32[4,6,66,129]{3,2,1,0:T(8,128)S(1)} %get-tuple-element.86, f32[4,6,65,128]{3,2,1,0:T(8,128)S(1)} %get-tuple-element.92, f32[4,6,66,129]{3,2,1,0:T(8,128)S(1)} %get-tuple-element.85, f32[4,1,64,128]{3,2,1,0:T(8,128)S(1)} %collective-permute-done.7, f32[4,4,64,128]{3,2,1,0:T(8,128)S(1)} %slice_divide_fusion.1, ...), kind=kLoop, calls=%fused_computation.277 | loop fusion | flops 7340032 | bytes 17563648 | tf_op jit(solution)/shard_map/mul | solution.py:70
  82.4 6.5 %collective-permute-done.12 = f32[7,1,64,128]{3,2,1,0:T(8,128)S(1)} collective-permute-done((f32[7,1,64,128]{3,2,1,0:T(8,128)S(1)}, f32[7,1,64,128]{3,2,1,0:T(8,128)S(1)}, u32[]{:S(2)}, u32[]{:S(2)}) %collective-permute-start.12) | collective-permute-done | bytes 229408 | tf_op jit(solution)/shard_map/ppermute | solution.py:15
  88.9 2.7 %collective-permute-done.13 = f32[7,1,64,128]{3,2,1,0:T(8,128)S(1)} collective-permute-done((f32[7,1,64,128]{3,2,1,0:T(8,128)S(1)}, f32[7,1,64,128]{3,2,1,0:T(8,128)S(1)}, u32[]{:S(2)}, u32[]{:S(2)}) %collective-permute-start.13) | collective-permute-done | bytes 229408 | tf_op jit(solution)/shard_map/ppermute | solution.py:18
  92.0 1.9 %collective-permute-start.14 = (f32[7,6,1,128]{3,0,2,1:T(8,128)S(1)}, f32[7,6,1,128]{3,0,2,1:T(8,128)S(1)}, u32[]{:S(2)}, u32[]{:S(2)}) collective-permute-start(f32[7,6,1,128]{3,0,2,1:T(8,128)S(1)} %copy.336), channel_id=1, source_target_pairs={{0,4},{4,8},{8,12},{12,0},{1,5},{5,9},{9,13},{13,1},{2,6},{6,10},{... | collective-permute-start | bytes 64520 | tf_op jit(solution)/shard_map/ppermute | solution.py:15
  95.7 1.9 %collective-permute-done.14 = f32[7,6,1,128]{3,0,2,1:T(8,128)S(1)} collective-permute-done((f32[7,6,1,128]{3,0,2,1:T(8,128)S(1)}, f32[7,6,1,128]{3,0,2,1:T(8,128)S(1)}, u32[]{:S(2)}, u32[]{:S(2)}) %collective-permute-start.14) | collective-permute-done | bytes 21536 | tf_op jit(solution)/shard_map/ppermute | solution.py:15
  99.5 2.6 %copy.318 = f32[7,6,66,1]{2,0,3,1:T(8,128)} copy(f32[7,6,66,1]{3,2,1,0:T(8,128)} %get-tuple-element.49) | data formatting | bytes 22176 | tf_op jit(solution)/shard_map/slice | solution.py:18
  106.7 2.5 %copy.319 = f32[7,6,66,1]{3,2,1,0:T(8,128)} copy(f32[7,6,66,1]{2,0,3,1:T(8,128)} %collective-permute-done.16) | data formatting | bytes 22176 | tf_op jit(solution)/shard_map/ppermute | solution.py:18
  111.0 6.1 %fusion.19 = (f32[7,6,66,129]{3,2,1,0:T(8,128)S(1)}, f32[7,6,66,129]{3,2,1,0:T(8,128)S(1)}) fusion(f32[1,4,64,128]{3,2,1,0:T(8,128)S(1)} %get-tuple-element.124, f32[1,4,64,128]{3,2,1,0:T(8,128)S(1)} %get-tuple-element.125, f32[1,4,64,128]{3,2,1,0:T(8,128)S(1)} %get-tuple-element.127, f32[7,6,66,1]{3,2,1,0:T(8,128)} %copy.319, ...), kind=kLoop, calls=%fused_computation.31 | loop fusion | flops 5721408 | bytes 4302144 | tf_op jit(solution)/shard_map/concatenate | solution.py:19
  119.4 2.9 %fusion.75 = f32[5,4,64,128]{3,2,1,0:T(8,128)S(1)} fusion(f32[1,4,64,128]{3,2,1,0:T(8,128)S(1)} %get-tuple-element.127, f32[7,6,66,129]{3,2,1,0:T(8,128)S(1)} %get-tuple-element.60, f32[7,6,65,128]{3,2,1,0:T(8,128)S(1)} %copy-done.1, f32[7,6,66,129]{3,2,1,0:T(8,128)S(1)} %get-tuple-element.59, f32[7,5,64,128]{3,2,1,0:T(8,128)S(1)} %copy-done.7, ...), kind=kLoop, calls=%fused_computation.141 | loop fusion | flops 8683520 | bytes 21757952 | tf_op jit(solution)/shard_map/add | solution.py:48
  124.5 4.3 %collective-permute-done.18 = f32[4,1,64,128]{3,2,1,0:T(8,128)S(1)} collective-permute-done((f32[4,1,64,128]{3,2,1,0:T(8,128)S(1)}, f32[4,1,64,128]{3,2,1,0:T(8,128)S(1)}, u32[]{:S(2)}, u32[]{:S(2)}) %collective-permute-start.18) | collective-permute-done | bytes 131104 | tf_op jit(solution)/shard_map/ppermute | solution.py:15
  128.9 2.6 %collective-permute-done.19 = f32[4,1,64,128]{3,2,1,0:T(8,128)S(1)} collective-permute-done((f32[4,1,64,128]{3,2,1,0:T(8,128)S(1)}, f32[4,1,64,128]{3,2,1,0:T(8,128)S(1)}, u32[]{:S(2)}, u32[]{:S(2)}) %collective-permute-start.19) | collective-permute-done | bytes 131104 | tf_op jit(solution)/shard_map/ppermute | solution.py:18
  131.5 2.0 %collective-permute-start.20 = (f32[4,6,1,128]{3,1,2,0:T(8,128)S(1)}, f32[4,6,1,128]{3,1,2,0:T(8,128)S(1)}, u32[]{:S(2)}, u32[]{:S(2)}) collective-permute-start(f32[4,6,1,128]{3,1,2,0:T(8,128)S(1)} %copy.324), channel_id=1, source_target_pairs={{0,4},{4,8},{8,12},{12,0},{1,5},{5,9},{9,13},{13,1},{2,6},{6,10},{... | collective-permute-start | bytes 36872 | tf_op jit(solution)/shard_map/ppermute | solution.py:15
  135.3 1.9 %collective-permute-done.20 = f32[4,6,1,128]{3,1,2,0:T(8,128)S(1)} collective-permute-done((f32[4,6,1,128]{3,1,2,0:T(8,128)S(1)}, f32[4,6,1,128]{3,1,2,0:T(8,128)S(1)}, u32[]{:S(2)}, u32[]{:S(2)}) %collective-permute-start.20) | collective-permute-done | bytes 12320 | tf_op jit(solution)/shard_map/ppermute | solution.py:15
  139.1 2.8 %collective-permute-done.22 = f32[4,6,66,1]{2,1,3,0:T(8,128)S(1)} collective-permute-done((f32[4,6,66,1]{2,1,3,0:T(8,128)S(1)}, f32[4,6,66,1]{2,1,3,0:T(8,128)S(1)}, u32[]{:S(2)}, u32[]{:S(2)}) %collective-permute-start.22) | collective-permute-done | bytes 6368 | tf_op jit(solution)/shard_map/ppermute | solution.py:15
  144.7 2.4 %maximum_maximum_fusion.1 = (f32[4,6,66,129]{3,2,1,0:T(8,128)S(1)}, f32[4,6,66,129]{3,2,1,0:T(8,128)S(1)}) fusion(f32[4,6,1,128]{3,2,1,0:T(1,128)S(1)} %copy.327, f32[4,1,64,128]{3,2,1,0:T(8,128)S(1)} %collective-permute-done.19, f32[4,4,64,128]{3,2,1,0:T(8,128)S(1)} %slice_divide_fusion, f32[4,1,64,128]{3,2,1,0:T(8,128)S(1)} %collective-permute-done.18, ...), kind=kLoop, calls=%fused_computation.58 | loop fusion | flops 2043360 | bytes 2458368 | tf_op jit(solution)/shard_map/concatenate | solution.py:19
  147.4 3.2 %fusion.101 = f32[4,4,64,128]{3,2,1,0:T(8,128)} fusion(f32[4,6,66,129]{3,2,1,0:T(8,128)S(1)} %get-tuple-element.84, f32[4,6,65,128]{3,2,1,0:T(8,128)S(1)} %get-tuple-element.88, f32[4,6,66,129]{3,2,1,0:T(8,128)S(1)} %get-tuple-element.83, f32[4,1,64,128]{3,2,1,0:T(8,128)S(1)} %collective-permute-done.19, f32[4,4,64,128]{3,2,1,0:T(8,128)S(1)} %slice_divide_fusion, ...), kind=kLoop, calls=%fused_computation.220 | loop fusion | flops 7208960 | bytes 17432576 | tf_op jit(solution)/shard_map/div | solution.py:83
  (256 shorter events, 47.0 us)
Async XLA Ops:
  0.9 3.4 %copy-start.66 = (f32[4,64,128]{2,1,0:T(8,128)}, f32[4,64,128]{2,1,0:T(8,128)S(1)}, u32[]{:S(2)}) copy-start(f32[4,64,128]{2,1,0:T(8,128)S(1)} %get-tuple-element.126) | copy-start | bytes 393220
  4.6 9.5 %collective-permute-start = (f32[7,1,64,128]{3,2,1,0:T(8,128)S(1)}, f32[7,1,64,128]{3,2,1,0:T(8,128)S(1)}, u32[]{:S(2)}, u32[]{:S(2)}) collective-permute-start(f32[7,1,64,128]{3,2,1,0:T(8,128)S(1)} %get-tuple-element.77), channel_id=1, source_target_pairs={{0,16},{16,0},{1,17},{17,1},{2,18},{18,2},{3,19},{19,3},{4,20},{20... | collective-permute-start | bytes 688136 | tf_op jit(solution)/shard_map/ppermute | solution.py:15
  7.6 10.5 %collective-permute-start.1 = (f32[7,1,64,128]{3,2,1,0:T(8,128)S(1)}, f32[7,1,64,128]{3,2,1,0:T(8,128)S(1)}, u32[]{:S(2)}, u32[]{:S(2)}) collective-permute-start(f32[7,1,64,128]{3,2,1,0:T(8,128)S(1)} %get-tuple-element.78), channel_id=1, source_target_pairs={{16,0},{0,16},{17,1},{1,17},{18,2},{2,18},{19,3},{3,19},{20,4},{4,... | collective-permute-start | bytes 688136 | tf_op jit(solution)/shard_map/ppermute | solution.py:18
  18.3 5.4 %collective-permute-start.3 = (f32[7,6,1,128]{3,0,2,1:T(8,128)S(1)}, f32[7,6,1,128]{3,0,2,1:T(8,128)S(1)}, u32[]{:S(2)}, u32[]{:S(2)}) collective-permute-start(f32[7,6,1,128]{3,0,2,1:T(8,128)S(1)} %copy.335), channel_id=1, source_target_pairs={{4,0},{8,4},{12,8},{0,12},{5,1},{9,5},{13,9},{1,13},{6,2},{10,6},{... | collective-permute-start | bytes 64520 | tf_op jit(solution)/shard_map/ppermute | solution.py:18
  22.2 5.6 %collective-permute-start.2 = (f32[7,6,1,128]{3,0,2,1:T(8,128)S(1)}, f32[7,6,1,128]{3,0,2,1:T(8,128)S(1)}, u32[]{:S(2)}, u32[]{:S(2)}) collective-permute-start(f32[7,6,1,128]{3,0,2,1:T(8,128)S(1)} %copy.334), channel_id=1, source_target_pairs={{0,4},{4,8},{8,12},{12,0},{1,5},{5,9},{9,13},{13,1},{2,6},{6,10},{... | collective-permute-start | bytes 64520 | tf_op jit(solution)/shard_map/ppermute | solution.py:15
  22.5 5.4 %copy-start.10 = (f32[7,5,64,128]{3,2,1,0:T(8,128)}, f32[7,5,64,128]{3,2,1,0:T(8,128)S(1)}, u32[]{:S(2)}) copy-start(f32[7,5,64,128]{3,2,1,0:T(8,128)S(1)} %get-tuple-element.76) | copy-start | bytes 3440644
  22.5 5.4 %copy-start.8 = (f32[7,5,64,128]{3,2,1,0:T(8,128)}, f32[7,5,64,128]{3,2,1,0:T(8,128)S(1)}, u32[]{:S(2)}) copy-start(f32[7,5,64,128]{3,2,1,0:T(8,128)S(1)} %get-tuple-element.75) | copy-start | bytes 3440644
  32.9 6.5 %collective-permute-start.5 = (f32[7,6,66,1]{2,0,3,1:T(8,128)S(1)}, f32[7,6,66,1]{2,0,3,1:T(8,128)S(1)}, u32[]{:S(2)}, u32[]{:S(2)}) collective-permute-start(f32[7,6,66,1]{2,0,3,1:T(8,128)S(1)} %copy.301), channel_id=1, source_target_pairs={{0,1},{1,2},{2,3},{3,0},{4,5},{5,6},{6,7},{7,4},{8,9},{9,10},{10,1... | collective-permute-start | bytes 33272 | tf_op jit(solution)/shard_map/ppermute | solution.py:15
  33.0 4.0 %collective-permute-start.4 = (f32[7,6,66,1]{2,0,3,1:T(8,128)}, f32[7,6,66,1]{2,0,3,1:T(8,128)}, u32[]{:S(2)}, u32[]{:S(2)}) collective-permute-start(f32[7,6,66,1]{2,0,3,1:T(8,128)} %copy.298), channel_id=1, source_target_pairs={{1,0},{2,1},{3,2},{0,3},{5,4},{6,5},{7,6},{4,7},{9,8},{10,9},{11,1... | collective-permute-start | bytes 33272 | tf_op jit(solution)/shard_map/ppermute | solution.py:18
  52.6 6.2 %collective-permute-start.6 = (f32[4,1,64,128]{3,2,1,0:T(8,128)S(1)}, f32[4,1,64,128]{3,2,1,0:T(8,128)S(1)}, u32[]{:S(2)}, u32[]{:S(2)}) collective-permute-start(f32[4,1,64,128]{3,2,1,0:T(8,128)S(1)} %get-tuple-element.97), channel_id=1, source_target_pairs={{0,16},{16,0},{1,17},{17,1},{2,18},{18,2},{3,19},{19,3},{4,20},{20... | collective-permute-start | bytes 393224 | tf_op jit(solution)/shard_map/ppermute | solution.py:15
  54.2 7.5 %collective-permute-start.7 = (f32[4,1,64,128]{3,2,1,0:T(8,128)S(1)}, f32[4,1,64,128]{3,2,1,0:T(8,128)S(1)}, u32[]{:S(2)}, u32[]{:S(2)}) collective-permute-start(f32[4,1,64,128]{3,2,1,0:T(8,128)S(1)} %get-tuple-element.98), channel_id=1, source_target_pairs={{16,0},{0,16},{17,1},{1,17},{18,2},{2,18},{19,3},{3,19},{20,4},{4,... | collective-permute-start | bytes 393224 | tf_op jit(solution)/shard_map/ppermute | solution.py:18
  61.7 3.8 %collective-permute-start.9 = (f32[4,6,1,128]{3,1,2,0:T(8,128)S(1)}, f32[4,6,1,128]{3,1,2,0:T(8,128)S(1)}, u32[]{:S(2)}, u32[]{:S(2)}) collective-permute-start(f32[4,6,1,128]{3,1,2,0:T(8,128)S(1)} %copy.305), channel_id=1, source_target_pairs={{4,0},{8,4},{12,8},{0,12},{5,1},{9,5},{13,9},{1,13},{6,2},{10,6},{... | collective-permute-start | bytes 36872 | tf_op jit(solution)/shard_map/ppermute | solution.py:18
  61.8 5.6 %collective-permute-start.8 = (f32[4,6,1,128]{3,1,2,0:T(8,128)S(1)}, f32[4,6,1,128]{3,1,2,0:T(8,128)S(1)}, u32[]{:S(2)}, u32[]{:S(2)}) collective-permute-start(f32[4,6,1,128]{3,1,2,0:T(8,128)S(1)} %copy.304), channel_id=1, source_target_pairs={{0,4},{4,8},{8,12},{12,0},{1,5},{5,9},{9,13},{13,1},{2,6},{6,10},{... | collective-permute-start | bytes 36872 | tf_op jit(solution)/shard_map/ppermute | solution.py:15
  68.6 4.8 %collective-permute-start.11 = (f32[4,6,66,1]{2,1,3,0:T(8,128)S(1)}, f32[4,6,66,1]{2,1,3,0:T(8,128)S(1)}, u32[]{:S(2)}, u32[]{:S(2)}) collective-permute-start(f32[4,6,66,1]{2,1,3,0:T(8,128)S(1)} %copy.311), channel_id=1, source_target_pairs={{1,0},{2,1},{3,2},{0,3},{5,4},{6,5},{7,6},{4,7},{9,8},{10,9},{11,1... | collective-permute-start | bytes 19016 | tf_op jit(solution)/shard_map/ppermute | solution.py:18
  68.7 3.4 %collective-permute-start.10 = (f32[4,6,66,1]{2,1,3,0:T(8,128)S(1)}, f32[4,6,66,1]{2,1,3,0:T(8,128)S(1)}, u32[]{:S(2)}, u32[]{:S(2)}) collective-permute-start(f32[4,6,66,1]{2,1,3,0:T(8,128)S(1)} %copy.308), channel_id=1, source_target_pairs={{0,1},{1,2},{2,3},{3,0},{4,5},{5,6},{6,7},{7,4},{8,9},{9,10},{10,1... | collective-permute-start | bytes 19016 | tf_op jit(solution)/shard_map/ppermute | solution.py:15
  74.7 2.7 %copy-start.20 = (f32[4,64,128]{2,1,0:T(8,128)S(1)}, f32[4,64,128]{2,1,0:T(8,128)}, u32[]{:S(2)}) copy-start(f32[4,64,128]{2,1,0:T(8,128)} %get-tuple-element.103) | copy-start | bytes 393220
  74.7 2.7 %copy-start.22 = (f32[4,64,128]{2,1,0:T(8,128)S(1)}, f32[4,64,128]{2,1,0:T(8,128)}, u32[]{:S(2)}) copy-start(f32[4,64,128]{2,1,0:T(8,128)} %get-tuple-element.104) | copy-start | bytes 393220
  74.7 2.7 %copy-start.24 = (f32[4,64,128]{2,1,0:T(8,128)S(1)}, f32[4,64,128]{2,1,0:T(8,128)}, u32[]{:S(2)}) copy-start(f32[4,64,128]{2,1,0:T(8,128)} %get-tuple-element.105) | copy-start | bytes 393220
  80.4 8.5 %collective-permute-start.12 = (f32[7,1,64,128]{3,2,1,0:T(8,128)S(1)}, f32[7,1,64,128]{3,2,1,0:T(8,128)S(1)}, u32[]{:S(2)}, u32[]{:S(2)}) collective-permute-start(f32[7,1,64,128]{3,2,1,0:T(8,128)S(1)} %get-tuple-element.73), channel_id=1, source_target_pairs={{0,16},{16,0},{1,17},{17,1},{2,18},{18,2},{3,19},{19,3},{4,20},{20... | collective-permute-start | bytes 688136 | tf_op jit(solution)/shard_map/ppermute | solution.py:15
  81.9 9.7 %collective-permute-start.13 = (f32[7,1,64,128]{3,2,1,0:T(8,128)S(1)}, f32[7,1,64,128]{3,2,1,0:T(8,128)S(1)}, u32[]{:S(2)}, u32[]{:S(2)}) collective-permute-start(f32[7,1,64,128]{3,2,1,0:T(8,128)S(1)} %get-tuple-element.74), channel_id=1, source_target_pairs={{16,0},{0,16},{17,1},{1,17},{18,2},{2,18},{19,3},{3,19},{20,4},{4,... | collective-permute-start | bytes 688136 | tf_op jit(solution)/shard_map/ppermute | solution.py:18
  91.7 3.9 %collective-permute-start.15 = (f32[7,6,1,128]{3,0,2,1:T(8,128)S(1)}, f32[7,6,1,128]{3,0,2,1:T(8,128)S(1)}, u32[]{:S(2)}, u32[]{:S(2)}) collective-permute-start(f32[7,6,1,128]{3,0,2,1:T(8,128)S(1)} %copy.337), channel_id=1, source_target_pairs={{4,0},{8,4},{12,8},{0,12},{5,1},{9,5},{13,9},{1,13},{6,2},{10,6},{... | collective-permute-start | bytes 64520 | tf_op jit(solution)/shard_map/ppermute | solution.py:18
  92.0 5.6 %collective-permute-start.14 = (f32[7,6,1,128]{3,0,2,1:T(8,128)S(1)}, f32[7,6,1,128]{3,0,2,1:T(8,128)S(1)}, u32[]{:S(2)}, u32[]{:S(2)}) collective-permute-start(f32[7,6,1,128]{3,0,2,1:T(8,128)S(1)} %copy.336), channel_id=1, source_target_pairs={{0,4},{4,8},{8,12},{12,0},{1,5},{5,9},{9,13},{13,1},{2,6},{6,10},{... | collective-permute-start | bytes 64520 | tf_op jit(solution)/shard_map/ppermute | solution.py:15
  94.1 3.5 %copy-start.6 = (f32[7,5,64,128]{3,2,1,0:T(8,128)}, f32[7,5,64,128]{3,2,1,0:T(8,128)S(1)}, u32[]{:S(2)}) copy-start(f32[7,5,64,128]{3,2,1,0:T(8,128)S(1)} %get-tuple-element.72) | copy-start | bytes 3440644
  94.1 3.5 %copy-start.4 = (f32[7,5,64,128]{3,2,1,0:T(8,128)}, f32[7,5,64,128]{3,2,1,0:T(8,128)S(1)}, u32[]{:S(2)}) copy-start(f32[7,5,64,128]{3,2,1,0:T(8,128)S(1)} %get-tuple-element.71) | copy-start | bytes 3440644
  102.7 6.5 %collective-permute-start.17 = (f32[7,6,66,1]{2,0,3,1:T(8,128)S(1)}, f32[7,6,66,1]{2,0,3,1:T(8,128)S(1)}, u32[]{:S(2)}, u32[]{:S(2)}) collective-permute-start(f32[7,6,66,1]{2,0,3,1:T(8,128)S(1)} %copy.321), channel_id=1, source_target_pairs={{0,1},{1,2},{2,3},{3,0},{4,5},{5,6},{6,7},{7,4},{8,9},{9,10},{10,1... | collective-permute-start | bytes 33272 | tf_op jit(solution)/shard_map/ppermute | solution.py:15
  102.7 4.0 %collective-permute-start.16 = (f32[7,6,66,1]{2,0,3,1:T(8,128)}, f32[7,6,66,1]{2,0,3,1:T(8,128)}, u32[]{:S(2)}, u32[]{:S(2)}) collective-permute-start(f32[7,6,66,1]{2,0,3,1:T(8,128)} %copy.318), channel_id=1, source_target_pairs={{1,0},{2,1},{3,2},{0,3},{5,4},{6,5},{7,6},{4,7},{9,8},{10,9},{11,1... | collective-permute-start | bytes 33272 | tf_op jit(solution)/shard_map/ppermute | solution.py:18
  122.4 6.4 %collective-permute-start.18 = (f32[4,1,64,128]{3,2,1,0:T(8,128)S(1)}, f32[4,1,64,128]{3,2,1,0:T(8,128)S(1)}, u32[]{:S(2)}, u32[]{:S(2)}) collective-permute-start(f32[4,1,64,128]{3,2,1,0:T(8,128)S(1)} %get-tuple-element.95), channel_id=1, source_target_pairs={{0,16},{16,0},{1,17},{17,1},{2,18},{18,2},{3,19},{19,3},{4,20},{20... | collective-permute-start | bytes 393224 | tf_op jit(solution)/shard_map/ppermute | solution.py:15
  124.0 7.4 %collective-permute-start.19 = (f32[4,1,64,128]{3,2,1,0:T(8,128)S(1)}, f32[4,1,64,128]{3,2,1,0:T(8,128)S(1)}, u32[]{:S(2)}, u32[]{:S(2)}) collective-permute-start(f32[4,1,64,128]{3,2,1,0:T(8,128)S(1)} %get-tuple-element.96), channel_id=1, source_target_pairs={{16,0},{0,16},{17,1},{1,17},{18,2},{2,18},{19,3},{3,19},{20,4},{4,... | collective-permute-start | bytes 393224 | tf_op jit(solution)/shard_map/ppermute | solution.py:18
  131.5 3.8 %collective-permute-start.21 = (f32[4,6,1,128]{3,1,2,0:T(8,128)S(1)}, f32[4,6,1,128]{3,1,2,0:T(8,128)S(1)}, u32[]{:S(2)}, u32[]{:S(2)}) collective-permute-start(f32[4,6,1,128]{3,1,2,0:T(8,128)S(1)} %copy.325), channel_id=1, source_target_pairs={{4,0},{8,4},{12,8},{0,12},{5,1},{9,5},{13,9},{1,13},{6,2},{10,6},{... | collective-permute-start | bytes 36872 | tf_op jit(solution)/shard_map/ppermute | solution.py:18
  131.5 5.6 %collective-permute-start.20 = (f32[4,6,1,128]{3,1,2,0:T(8,128)S(1)}, f32[4,6,1,128]{3,1,2,0:T(8,128)S(1)}, u32[]{:S(2)}, u32[]{:S(2)}) collective-permute-start(f32[4,6,1,128]{3,1,2,0:T(8,128)S(1)} %copy.324), channel_id=1, source_target_pairs={{0,4},{4,8},{8,12},{12,0},{1,5},{5,9},{9,13},{13,1},{2,6},{6,10},{... | collective-permute-start | bytes 36872 | tf_op jit(solution)/shard_map/ppermute | solution.py:15
  138.4 4.8 %collective-permute-start.23 = (f32[4,6,66,1]{2,1,3,0:T(8,128)S(1)}, f32[4,6,66,1]{2,1,3,0:T(8,128)S(1)}, u32[]{:S(2)}, u32[]{:S(2)}) collective-permute-start(f32[4,6,66,1]{2,1,3,0:T(8,128)S(1)} %copy.331), channel_id=1, source_target_pairs={{1,0},{2,1},{3,2},{0,3},{5,4},{6,5},{7,6},{4,7},{9,8},{10,9},{11,1... | collective-permute-start | bytes 19016 | tf_op jit(solution)/shard_map/ppermute | solution.py:18
  138.4 3.4 %collective-permute-start.22 = (f32[4,6,66,1]{2,1,3,0:T(8,128)S(1)}, f32[4,6,66,1]{2,1,3,0:T(8,128)S(1)}, u32[]{:S(2)}, u32[]{:S(2)}) collective-permute-start(f32[4,6,66,1]{2,1,3,0:T(8,128)S(1)} %copy.328), channel_id=1, source_target_pairs={{0,1},{1,2},{2,3},{3,0},{4,5},{5,6},{6,7},{7,4},{8,9},{9,10},{10,1... | collective-permute-start | bytes 19016 | tf_op jit(solution)/shard_map/ppermute | solution.py:15
  (70 other events, 170.2 us)
where the time goes:
time: 151 us
  waiting for transfers between devices  52.8 us (35%)
  other arithmetic  41.1 us (27%)
  local copies, waits for them, and re-layouts  31.1 us (21%)
  starting transfers between devices  24.1 us (16%)
    ppermute x12, waiting for transfers between devices, extended(): lax.ppermute(lax.slice_in_dim(block, block.shape[dim] - width, None, axis...  36.6 us
    concatenate x16, other arithmetic, extended(): block = jnp.concatenate([low, block, high], axis=dim)  19.1 us
    ppermute x12, waiting for transfers between devices, extended(): lax.ppermute(lax.slice_in_dim(block, 0, width, axis=dim), axis, backward)  16.2 us
    ppermute x12, starting transfers between devices, extended(): lax.ppermute(lax.slice_in_dim(block, block.shape[dim] - width, None, axis...  14.6 us
    ppermute x12, starting transfers between devices, extended(): lax.ppermute(lax.slice_in_dim(block, 0, width, axis=dim), axis, backward)  9.48 us
    slice x8, local copies, waits for them, and re-layouts, extended(): lax.slice_in_dim(block, 0, width, axis=dim)  9.39 us
    ppermute x8, local copies, waits for them, and re-layouts, extended(): lax.ppermute(lax.slice_in_dim(block, 0, width, axis=dim), axis, backward)  7.63 us
    ppermute x8, local copies, waits for them, and re-layouts, extended(): lax.ppermute(lax.slice_in_dim(block, block.shape[dim] - width, None, axis...  6.29 us
  transfers between devices with their start and end apart: 24, of which 18 were waited for; matrix products, arithmetic and copies ran while one was open for 9% of the time, Pallas kernels for 0%

commit v1 on v0

v1 whole, which is shorter than its diff:
```python
import functools

import jax
import jax.numpy as jnp
from jax import lax
from jax.experimental import pallas as pl
from jax.experimental.pallas import tpu as pltpu
from jax.sharding import PartitionSpec as P

PASSES = 2
HALO = 2 * PASSES
LANES = 128
GROUP = 16
TOP = 8
LOW_BITS = 14

VMEM = pl.BlockSpec(memory_space=pltpu.VMEM)
PARAMS = pltpu.CompilerParams(vmem_limit_bytes=60 * 2**20)


def offsets():
    return [(dx, dy, dz) for dx in (-1, 0, 1) for dy in (-1, 0, 1) for dz in (-1, 0, 1)]


def bit_of(dx, dy, dz):
    return 9 * (dx + 1) + 3 * (dy + 1) + (dz + 1)


def slot_of(dx, dy, dz):
    index = bit_of(dx, dy, dz)
    return index if index < 13 else index - 1


def roll(value, shift):
    shift = shift % LANES
    return value if shift == 0 else pltpu.roll(value, shift, 1)


def ring(axis, step):
    count = lax.axis_size(axis)
    return [(i, (i + step) % count) for i in range(count)]


def pack_kernel(fields, code, flag, bits, ints, zlo, zhi, ylo, yhi):
    count, sx, sy, sz = fields.shape
    lane = lax.broadcasted_iota(jnp.int32, (sy, LANES), 1)
    low_side = jnp.zeros((sy, LANES), jnp.float32)
    high_side = jnp.zeros((sy, LANES), jnp.float32)
    for p in range(sx):
        active = bits[p] * flag[p]
        ints[0, p] = code[p]
        ints[1, p] = active
        planes = [fields[f, p] for f in range(count)]
        planes.append(code[p].astype(jnp.float32))
        planes.append(jnp.bitwise_and(active, 2**LOW_BITS - 1).astype(jnp.float32))
        planes.append(jnp.right_shift(active, LOW_BITS).astype(jnp.float32))
        for a, plane in enumerate(planes):
            row = (a * sx + p) * HALO
            ylo[pl.ds(row, HALO), :] = plane[:HALO]
            yhi[pl.ds(row, HALO), :] = plane[sy - HALO :]
            first = row
            here = (lane >= first) & (lane < first + HALO)
            low_side = jnp.where(here, roll(plane, first), low_side)
            high_side = jnp.where(here, roll(plane, first + HALO), high_side)
    zlo[...] = low_side
    zhi[...] = high_side


def pack(fields, code, flag, bits):
    count, sx, sy, sz = fields.shape
    rows = (count + 3) * sx * HALO
    f32 = jnp.float32
    return pl.pallas_call(
        pack_kernel,
        out_shape=(
            jax.ShapeDtypeStruct((2, sx, sy, sz), jnp.int32),
            jax.ShapeDtypeStruct((sy, LANES), f32),
            jax.ShapeDtypeStruct((sy, LANES), f32),
            jax.ShapeDtypeStruct((rows, LANES), f32),
            jax.ShapeDtypeStruct((rows, LANES), f32),
        ),
        in_specs=[VMEM] * 4,
        out_specs=(VMEM,) * 5,
        compiler_params=PARAMS,
        name="pack",
    )(fields, code, flag, bits)


class Box:
    def __init__(self, count, sx, sy, blocks):
        self.count, self.sx, self.sy, self.blocks = count, sx, sy, blocks
        self.planes = sx * blocks
        self.tiles = -(-self.planes * GROUP // LANES)
        self.rows = sy + 2 * TOP
        self.steps = -(-(sy + 2 * HALO) // 8)

    def near(self, reach):
        wanted = range(-reach, self.sx + reach)
        return sorted({x % self.planes for x in wanted})


def lane_index():
    return lax.broadcasted_iota(jnp.int32, (8, LANES), 1)


def fill(box, main_of, low_of, high_of, main, strip):
    lane = lane_index()

    def step(t, _):
        r = t * 8 + TOP - HALO
        out = [jnp.zeros((8, LANES), jnp.float32) for _ in range(box.tiles)]
        for b in range(box.blocks):
            lows, highs = low_of(b, r), high_of(b, r)
            for p in range(box.sx):
                x = b * box.sx + p
                tile, first = divmod(x * GROUP, LANES)
                plane = main_of(x, r)
                for c, value in (
                    (0, lows[p]),
                    (HALO, (plane, 0)),
                    (2 * HALO, (plane, LANES - HALO)),
                    (3 * HALO, highs[p]),
                ):
                    data, lane0 = value
                    at = first + c
                    here = (lane >= at) & (lane < at + HALO)
                    out[tile] = jnp.where(here, roll(data, at - lane0), out[tile])
        for tile in range(box.tiles):
            strip[tile, pl.ds(r, 8), :] = out[tile].astype(strip.dtype)
        return 0

    lax.fori_loop(0, box.steps, step, 0)


def roll_groups(values, shift):
    count = len(values)
    rolled = [roll(v, shift) for v in values]
    if count == 1 or shift == 0:
        return rolled
    lane = lane_index()
    if shift > 0:
        return [jnp.where(lane < shift, rolled[(k - 1) % count], rolled[k]) for k in range(count)]
    return [jnp.where(lane >= LANES + shift, rolled[(k + 1) % count], rolled[k]) for k in range(count)]


def add(left, right):
    return right if left is None else left + right


def strip_scatter(box, masks, value, r):
    parts = {}
    for dz in (-1, 0, 1):
        total = [None] * box.tiles
        for dx in (-1, 0, 1):
            sums = [None] * box.tiles
            for dy in (-1, 0, 1):
                for k in range(box.tiles):
                    piece = value[k, pl.ds(r - dy, 8), :]
                    if (dx, dy, dz) != (0, 0, 0):
                        piece = piece * masks[slot_of(dx, dy, dz), k, pl.ds(r - dy, 8), :]
                    sums[k] = add(sums[k], piece)
            sums = roll_groups(sums, GROUP * dx)
            total = [add(t, s) for t, s in zip(total, sums)]
        parts[dz] = total
    up = roll_groups(parts[1], 1)
    down = roll_groups(parts[-1], -1)
    return parts, [a + b + c for a, b, c in zip(parts[0], up, down)]


def from_strip(tiles, x, column, lane):
    tile, first = divmod(x * GROUP + column, LANES)
    return roll(tiles[tile], lane - first)


LAST = HALO - 1
NEXT = 3 * HALO


def main_scatter(box, masks, value, xs, r, parts):
    lane = lane_index()
    count = len(value)
    result = [[None] * len(xs) for _ in range(count)]
    for dz in (0, 1, -1):
        sums = [[None] * len(xs) for _ in range(count)]
        for dy in (-1, 0, 1):
            cells = {}
            for dx in (-1, 0, 1):
                for i, x in enumerate(xs):
                    source = (x - dx) % box.planes
                    if source not in cells:
                        cells[source] = [value[f][source, pl.ds(r - dy, 8), :] for f in range(count)]
                    mask = None
                    if (dx, dy, dz) != (0, 0, 0):
                        mask = masks[slot_of(dx, dy, dz), source, pl.ds(r - dy, 8), :]
                    for f in range(count):
                        piece = cells[source][f]
                        sums[f][i] = add(sums[f][i], piece if mask is None else piece * mask)
        for f in range(count):
            for i, x in enumerate(xs):
                piece = sums[f][i]
                if dz == 1:
                    piece = jnp.where(lane == 0, from_strip(parts[f][1], x, LAST, 0), roll(piece, 1))
                elif dz == -1:
                    piece = jnp.where(lane == LANES - 1, from_strip(parts[f][-1], x, NEXT, LANES - 1), roll(piece, -1))
                result[f][i] = add(result[f][i], piece)
    return result


def main_gather(box, masks, value, xs, r):
    count = len(value)
    sums = [[None] * len(xs) for _ in range(count)]
    for dz in (-1, 0, 1):
        for dy in (-1, 0, 1):
            cells = {}
            for dx in (-1, 0, 1):
                for i, x in enumerate(xs):
                    source = (x + dx) % box.planes
                    if source not in cells:
                        cells[source] = [value[f][dz + 1, source, pl.ds(r + dy, 8), :] for f in range(count)]
                    mask = None
                    if (dx, dy, dz) != (0, 0, 0):
                        mask = masks[slot_of(dx, dy, dz), x, pl.ds(r, 8), :]
                    for f in range(count):
                        piece = cells[source][f]
                        sums[f][i] = add(sums[f][i], piece if mask is None else piece * mask)
    return sums


def chunks(xs, size=4):
    return [xs[i : i + size] for i in range(0, len(xs), size)]


def scatter_stage(box, refs, group, xs):
    masks, smasks, inverse, sinverse = refs["mask"], refs["smask"], refs["inv"], refs["sinv"]
    lane = lane_index()

    def step(t, _):
        r = t * 8 + TOP - HALO
        parts, shats = [], []
        for f in group:
            part, totals = strip_scatter(box, smasks, refs["sw"].at[f], r)
            shat = [total * sinverse[k, pl.ds(r, 8), :] for k, total in enumerate(totals)]
            parts.append(part)
            shats.append(shat)
            for dx in (-1, 0, 1):
                for dz in (-1, 0, 1):
                    shifted = roll_groups(roll_groups(shat, -GROUP * dx), -dz)
                    for k in range(box.tiles):
                        refs["shat"][f, 3 * (dx + 1) + dz + 1, k, pl.ds(r, 8), :] = shifted[k]
        for part_xs in chunks(xs):
            totals = main_scatter(box, masks, [refs["w"].at[f] for f in group], part_xs, r, parts)
            for g, f in enumerate(group):
                for i, x in enumerate(part_xs):
                    hat = totals[g][i] * inverse[x, pl.ds(r, 8), :]
                    refs["hat"][f, 1, x, pl.ds(r, 8), :] = hat
                    refs["hat"][f, 0, x, pl.ds(r, 8), :] = jnp.where(
                        lane == 0, from_strip(shats[g], x, LAST, 0), roll(hat, 1)
                    )
                    refs["hat"][f, 2, x, pl.ds(r, 8), :] = jnp.where(
                        lane == LANES - 1, from_strip(shats[g], x, NEXT, LANES - 1), roll(hat, -1)
                    )
        return 0

    lax.fori_loop(0, box.steps, step, 0)


def gather_stage(box, refs, group, xs, out):
    masks, smasks = refs["mask"], refs["smask"]
    first = TOP - HALO if out is None else TOP
    steps = box.steps if out is None else box.sy // 8

    def step(t, _):
        r = t * 8 + first
        for f in group if out is None else ():
            sums = [None] * box.tiles
            for dx, dy, dz in offsets():
                for k in range(box.tiles):
                    piece = refs["shat"][f, 3 * (dx + 1) + dz + 1, k, pl.ds(r + dy, 8), :]
                    if (dx, dy, dz) != (0, 0, 0):
                        piece = piece * smasks[slot_of(dx, dy, dz), k, pl.ds(r, 8), :]
                    sums[k] = add(sums[k], piece)
            for k in range(box.tiles):
                refs["sw"][f, k, pl.ds(r, 8), :] = sums[k] * refs["sscale"][k, pl.ds(r, 8), :]
        for part_xs in chunks(xs):
            sums = main_gather(box, masks, [refs["hat"].at[f] for f in group], part_xs, r)
            for g, f in enumerate(group):
                for i, x in enumerate(part_xs):
                    if out is None:
                        refs["w"][f, x, pl.ds(r, 8), :] = sums[g][i] * refs["scale"][x, pl.ds(r, 8), :]
                    else:
                        out[f, x, pl.ds(t * 8, 8), :] = sums[g][i] * refs["icount"][x, pl.ds(r, 8), :]
        return 0

    lax.fori_loop(0, steps, step, 0)


def masks_stage(box, refs):
    def one(active, kappa, mask, inv_count, scale, index, r):
        count = None
        for dx, dy, dz in offsets():
            if (dx, dy, dz) == (0, 0, 0):
                continue
            bit = jnp.bitwise_and(jnp.right_shift(active, bit_of(dx, dy, dz)), 1).astype(jnp.float32)
            mask[slot_of(dx, dy, dz), index, pl.ds(r, 8), :] = bit
            count = add(count, bit)
        inverse = 1.0 / (count + 1.0)
        if inv_count is not None:
            inv_count[index, pl.ds(r, 8), :] = inverse
        scale[index, pl.ds(r, 8), :] = inverse * kappa

    def step(t, _):
        r = t * 8 + TOP - HALO
        for k in range(box.tiles):
            kappa = refs["skappa"][k, pl.ds(r, 8), :]
            one(refs["sactive"][k, pl.ds(r, 8), :], kappa, refs["smask"], None, refs["sscale"], k, r)
        for x in range(box.planes):
            kappa = refs["kappa"][x, pl.ds(r, 8), :]
            one(refs["active"][x, pl.ds(r, 8), :], kappa, refs["mask"], refs["icount"], refs["scale"], x, r)
        return 0

    lax.fori_loop(0, box.steps, step, 0)


def volume_stage(box, refs, xs):
    def step(t, _):
        r = t * 8 + TOP - HALO
        part, totals = strip_scatter(box, refs["smask"], refs["skappa"], r)
        for k in range(box.tiles):
            refs["sinv"][k, pl.ds(r, 8), :] = 1.0 / totals[k]
        for part_xs in chunks(xs):
            totals = main_scatter(box, refs["mask"], [refs["kappa"]], part_xs, r, [part])
            for i, x in enumerate(part_xs):
                refs["inv"][x, pl.ds(r, 8), :] = 1.0 / totals[0][i]
        return 0

    lax.fori_loop(0, box.steps, step, 0)


SCRATCH = ("mask", "smask", "inv", "sinv", "w", "sw", "hat", "shat", "icount", "scale", "sscale", "kappa", "skappa", "active", "sactive", "half", "shalf", "zbuf")


def scratch_shapes(box):
    p, k, r, n = box.planes, box.tiles, box.rows, box.count
    f32 = jnp.float32
    return [
        pltpu.VMEM((26, p, r, LANES), f32),
        pltpu.VMEM((26, k, r, LANES), f32),
        pltpu.VMEM((p, r, LANES), f32),
        pltpu.VMEM((k, r, LANES), f32),
        pltpu.VMEM((n, p, r, LANES), f32),
        pltpu.VMEM((n, k, r, LANES), f32),
        pltpu.VMEM((n, 3, p, r, LANES), f32),
        pltpu.VMEM((n, 9, k, r, LANES), f32),
        pltpu.VMEM((p, r, LANES), f32),
        pltpu.VMEM((p, r, LANES), f32),
        pltpu.VMEM((k, r, LANES), f32),
        pltpu.VMEM((p, r, LANES), f32),
        pltpu.VMEM((k, r, LANES), f32),
        pltpu.VMEM((p, r, LANES), jnp.int32),
        pltpu.VMEM((k, r, LANES), jnp.int32),
        pltpu.VMEM((2, p, r, LANES), f32),
        pltpu.VMEM((2, k, r, LANES), f32),
        pltpu.VMEM((2, box.blocks, r, LANES), f32),
    ]


def local_kernel(box, *refs):
    nb, sx, sy, count = box.blocks, box.sx, box.sy, box.count
    fields, refs = refs[:nb], refs[nb:]
    ints, refs = refs[:nb], refs[nb:]
    edges, refs = refs[:nb], refs[nb:]
    out, refs = refs[0], dict(zip(SCRATCH, refs[1:]))
    ymain = (count + 3) * sx * HALO
    ylow, yhigh = 2 * sy, 2 * sy + ymain + 2 * HALO
    own_rows, before, after = pl.ds(TOP, sy), pl.ds(TOP - HALO, HALO), pl.ds(TOP + sy, HALO)
    zbuf = refs["zbuf"]
    for b in range(nb):
        for side in range(2):
            zbuf[side, b, own_rows, :] = edges[b][pl.ds(side * sy, sy), :]
            zbuf[side, b, before, :] = edges[b][pl.ds(ylow + ymain + side * HALO, HALO), :]
            zbuf[side, b, after, :] = edges[b][pl.ds(yhigh + ymain + side * HALO, HALO), :]

    def halo_rows(target, a, x):
        b, p = divmod(x, sx)
        row = (a * sx + p) * HALO
        target[x, before, :] = edges[b][pl.ds(ylow + row, HALO), :]
        target[x, after, :] = edges[b][pl.ds(yhigh + row, HALO), :]

    def strips(a, main, strip):
        def side_of(side):
            def get(b, r):
                tile = zbuf[side, b, pl.ds(r, 8), :]
                return [(tile, (a * sx + p) * HALO) for p in range(sx)]

            return get

        fill(box, lambda x, r: main[x, pl.ds(r, 8), :], side_of(0), side_of(1), main, strip)

    half, shalf = refs["half"], refs["shalf"]
    for x in range(box.planes):
        b, p = divmod(x, sx)
        refs["kappa"][x, own_rows, :] = ints[b][0, p].astype(jnp.float32)
        active = ints[b][1, p]
        half[0, x, own_rows, :] = jnp.bitwise_and(active, 2**LOW_BITS - 1).astype(jnp.float32)
        half[1, x, own_rows, :] = jnp.right_shift(active, LOW_BITS).astype(jnp.float32)
        halo_rows(refs["kappa"], count, x)
        halo_rows(half.at[0], count + 1, x)
        halo_rows(half.at[1], count + 2, x)
    strips(count, refs["kappa"], refs["skappa"])
    for i in range(2):
        strips(count + 1 + i, half.at[i], shalf.at[i])

    def convert(t, _):
        rows = pl.ds(t * 8 + TOP - HALO, 8)
        for full, kappa, active, n in (
            (half, refs["kappa"], refs["active"], box.planes),
            (shalf, refs["skappa"], refs["sactive"], box.tiles),
        ):
            for x in range(n):
                kappa[x, rows, :] = kappa[x, rows, :] * 2.0**-20
                active[x, rows, :] = full[0, x, rows, :].astype(jnp.int32) + full[1, x, rows, :].astype(jnp.int32) * 2**LOW_BITS
        return 0

    lax.fori_loop(0, box.steps, convert, 0)
    masks_stage(box, refs)
    volume_stage(box, refs, box.near(HALO - 1))

    for f in range(count):
        w = refs["w"].at[f]
        for x in range(box.planes):
            b, p = divmod(x, sx)
            w[x, own_rows, :] = fields[b][f, p]
            halo_rows(w, f, x)
        strips(f, w, refs["sw"].at[f])

        def weigh(t, _, f=f):
            rows = pl.ds(t * 8 + TOP - HALO, 8)
            for x in range(box.planes):
                refs["w"][f, x, rows, :] = refs["w"][f, x, rows, :] * refs["kappa"][x, rows, :]
            for k in range(box.tiles):
                refs["sw"][f, k, rows, :] = refs["sw"][f, k, rows, :] * refs["skappa"][k, rows, :]
            return 0

        lax.fori_loop(0, box.steps, weigh, 0)

    for group in chunks(list(range(count)), 2):
        for step in range(PASSES):
            reach = HALO - 1 - 2 * step
            scatter_stage(box, refs, group, box.near(reach))
            gather_stage(box, refs, group, box.near(reach - 1), None if step < PASSES - 1 else out)


def local(box, fields, ints, edges):
    shape = fields[0].shape
    return pl.pallas_call(
        functools.partial(local_kernel, box),
        out_shape=jax.ShapeDtypeStruct(shape, jnp.float32),
        in_specs=[VMEM] * (3 * box.blocks),
        out_specs=VMEM,
        scratch_shapes=scratch_shapes(box),
        compiler_params=PARAMS,
        name="local",
    )(*fields, *ints, *edges)


def body(fields, volume_code, cut_flag, member_bits):
    count, sx, sy, sz = fields.shape
    size = lax.axis_size("gx")

    def from_x(value):
        if size == 1:
            return []
        if size == 2:
            return [lax.ppermute(value, "gx", ring("gx", 1))]
        return [lax.ppermute(value, "gx", ring("gx", -1)), lax.ppermute(value, "gx", ring("gx", 1))]

    ints, zlo, zhi, ylo, yhi = pack(fields, volume_code, cut_flag, member_bits)
    all_fields = [fields] + from_x(fields)
    all_ints = [ints] + from_x(ints)
    low = lax.ppermute(zhi, "gz", ring("gz", 1))
    high = lax.ppermute(zlo, "gz", ring("gz", -1))
    ylo = jnp.concatenate([ylo, low[:HALO], high[:HALO]])
    yhi = jnp.concatenate([yhi, low[sy - HALO :], high[sy - HALO :]])
    before = lax.ppermute(yhi, "gy", ring("gy", 1))
    after = lax.ppermute(ylo, "gy", ring("gy", -1))
    edge = jnp.concatenate([low, high, before, after])
    all_edges = [edge] + from_x(edge)
    box = Box(count, sx, sy, len(all_fields))
    return local(box, all_fields, all_ints, all_edges)


def solution(mesh):
    in_specs = (
        P(None, "gx", "gy", "gz"),
        P("gx", "gy", "gz"),
        P("gx", "gy", "gz"),
        P("gx", "gy", "gz"),
    )
    out_specs = P(None, "gx", "gy", "gz")
    return jax.shard_map(body, mesh=mesh, in_specs=in_specs, out_specs=out_specs, check_vma=False)
```

time: 151 us -> 60.7 us (0.40)
  other arithmetic: 41.1 us -> 0.84 us
  waiting for transfers between devices: 52.8 us -> 14.2 us
  Pallas kernels: 0 us -> 34.2 us
  local copies, waits for them, and re-layouts: 31.1 us -> 1.48 us
  starting transfers between devices: 24.1 us -> 9.33 us
    ppermute x24 -> x7, waiting for transfers between devices: 52.8 us -> 14.2 us  [the longest x3 8.89 us: from_x(): return [lax.ppermute(value, 'gx', ring('gx', 1))]]
    pallas_call x0 -> x2, Pallas kernels: none -> 34.2 us  [the longest x1 31.8 us: local(): pl.pallas_call(functools.partial(local_kernel, box), out_shape=jax.ShapeD...]
    concatenate x18 -> x2, other arithmetic: 19.2 us -> 0.84 us  [the longest x1 0.83 us: body(): yhi = jnp.concatenate([yhi, low[sy - HALO:], high[sy - HALO:]])]
    ppermute x24 -> x7, starting transfers between devices: 24.1 us -> 9.33 us  [the longest x3 3.57 us: from_x(): return [lax.ppermute(value, 'gx', ring('gx', 1))]]
    ppermute x16 -> x0, local copies, waits for them, and re-layouts: 13.9 us -> none  [the longest x8 7.63 us: extended(): lax.ppermute(lax.slice_in_dim(block, 0, width, axis=dim), axis, backward)]
    slice x22 -> x2, local copies, waits for them, and re-layouts: 12.2 us -> 0.01 us  [body(): ylo = jnp.concatenate([ylo, low[:HALO], high[:HALO]])]
    mul x11 -> x0, other arithmetic: 7.17 us -> none  [the longest x9 4.53 us: pulled_sums(): sums = sums + member[None] * piece[:5]]
    add x3 -> x0, other arithmetic: 6.96 us -> none  [the longest x2 5.84 us: pulled_sums(): sums = sums + member[None] * piece[:5]]
  transfers between devices with their start and end apart: 24 -> 7, of which waited for: 18 -> 5; matrix products, arithmetic and copies ran while one was open for 9% -> 1% of each run, Pallas kernels for 0% -> 0%
where the time goes in v1:
time: 60.7 us; the launch traced here: 60.1 us
  Pallas kernels  34.2 us (56%)
  waiting for transfers between devices  14.2 us (23%)
  starting transfers between devices  9.33 us (15%)
  local copies, waits for them, and re-layouts  1.48 us (2%)
  other arithmetic  0.84 us (1%)
    pallas_call x1, Pallas kernels, local(): pl.pallas_call(functools.partial(local_kernel, box), out_shape=jax.ShapeD...  31.8 us
    ppermute x3, waiting for transfers between devices, from_x(): return [lax.ppermute(value, 'gx', ring('gx', 1))]  8.89 us
    ppermute x3, starting transfers between devices, from_x(): return [lax.ppermute(value, 'gx', ring('gx', 1))]  3.57 us
    pallas_call x1, Pallas kernels, pack(): pl.pallas_call(pack_kernel, out_shape=(jax.ShapeDtypeStruct((2, sx, sy, s...  2.41 us
    ppermute x1, starting transfers between devices, body(): after = lax.ppermute(ylo, 'gy', ring('gy', -1))  2.3 us
    ppermute x1, waiting for transfers between devices, body(): before = lax.ppermute(yhi, 'gy', ring('gy', 1))  2.22 us
    ppermute x1, waiting for transfers between devices, body(): high = lax.ppermute(zlo, 'gz', ring('gz', -1))  1.62 us
    ppermute x1, starting transfers between devices, body(): before = lax.ppermute(yhi, 'gy', ring('gy', 1))  1.58 us
  transfers between devices with their start and end apart: 7, of which 5 were waited for; matrix products, arithmetic and copies ran while one was open for 1% of the time, Pallas kernels for 0%

profile of v1, /device:TPU:0, one launch (start us, length us, event | category | flops | bytes accessed | tf_op | source)
XLA Modules:
  0.0 60.1 jit_solution(10947415598392335402)
XLA Ops:
  0.0 0.0 copy-start
  0.0 2.4 %pack.1 = (s32[2,4,64,128]{3,2,1,0:T(8,128)}, f32[64,128]{1,0:T(8,128)}, f32[64,128]{1,0:T(8,128)}, f32[112,128]{1,0:T(8,128)}, f32[112,128]{1,0:T(8,128)}) custom-call(f32[4,4,64,128]{3,2,1,0:T(8,128)} %refs_0_.1, s32[4,64,128]{2,1,0:T(8,128)} %code.1, s32[4,64,128]{2,1,0:T(8,128)} %flag.1, s32[4,64,128]{2,1,0:T(8,128)} %bits.1), custom_call_target="tpu_custom_call" | custom-call | tf_op jit(solution)/shard_map/pack/pallas_call | solution.py:73
  2.4 0.5 collective-permute-start.2
  2.9 0.0 copy-done
  2.9 2.5 %collective-permute-start = (f32[4,4,64,128]{3,2,1,0:T(8,128)S(1)}, f32[4,4,64,128]{3,2,1,0:T(8,128)S(1)}, u32[]{:S(2)}, u32[]{:S(2)}) collective-permute-start(f32[4,4,64,128]{3,2,1,0:T(8,128)S(1)} %copy-done), channel_id=1, source_target_pairs={{0,16},{16,0},{1,17},{17,1},{2,18},{18,2},{3,19},{19,3},{4,20},{20... | collective-permute-start | bytes 1572872 | tf_op jit(solution)/shard_map/ppermute | solution.py:474
  5.5 1.4 %collective-permute-start.3 = (f32[64,128]{1,0:T(8,128)}, f32[64,128]{1,0:T(8,128)S(1)}, u32[]{:S(2)}, u32[]{:S(2)}) collective-permute-start(f32[64,128]{1,0:T(8,128)} %get-tuple-element.12), channel_id=1, source_target_pairs={{0,3},{1,0},{2,1},{3,2},{4,7},{5,4},{6,5},{7,6},{8,11},{9,8},{10,9... | collective-permute-start | bytes 98312 | tf_op jit(solution)/shard_map/ppermute | solution.py:481
  6.8 0.3 collective-permute-start.1
  7.1 0.0 collective-permute-done.2
  7.1 1.6 %collective-permute-done.3 = f32[64,128]{1,0:T(8,128)S(1)} collective-permute-done((f32[64,128]{1,0:T(8,128)}, f32[64,128]{1,0:T(8,128)S(1)}, u32[]{:S(2)}, u32[]{:S(2)}) %collective-permute-start.3) | collective-permute-done | bytes 32800 | tf_op jit(solution)/shard_map/ppermute | solution.py:481
  8.8 0.0 copy-start.5
  8.8 0.8 %pad_maximum_fusion = f32[120,128]{1,0:T(8,128)S(1)} fusion(f32[4,128]{1,0:T(4,128)S(1)} %get-tuple-element.18, f32[4,128]{1,0:T(4,128)S(1)} %get-tuple-element.16, f32[112,128]{1,0:T(8,128)} %get-tuple-element.13), kind=kLoop, calls=%fused_computation | loop fusion | flops 30720 | bytes 122880 | tf_op jit(solution)/shard_map/concatenate | solution.py:483
  9.6 1.6 %collective-permute-start.4 = (f32[120,128]{1,0:T(8,128)S(1)}, f32[120,128]{1,0:T(8,128)S(1)}, u32[]{:S(2)}, u32[]{:S(2)}) collective-permute-start(f32[120,128]{1,0:T(8,128)S(1)} %pad_maximum_fusion), channel_id=1, source_target_pairs={{0,4},{4,8},{8,12},{12,0},{1,5},{5,9},{9,13},{13,1},{2,6},{6,10},{... | collective-permute-start | bytes 184328 | tf_op jit(solution)/shard_map/ppermute | solution.py:484
  11.2 0.0 copy-done.5
  11.2 2.3 %collective-permute-start.5 = (f32[120,128]{1,0:T(8,128)S(1)}, f32[120,128]{1,0:T(8,128)S(1)}, u32[]{:S(2)}, u32[]{:S(2)}) collective-permute-start(f32[120,128]{1,0:T(8,128)S(1)} %pad_maximum_fusion.1), channel_id=1, source_target_pairs={{0,12},{4,0},{8,4},{12,8},{1,13},{5,1},{9,5},{13,9},{2,14},{6,2},{... | collective-permute-start | bytes 184328 | tf_op jit(solution)/shard_map/ppermute | solution.py:485
  13.5 2.2 %collective-permute-done.4 = f32[120,128]{1,0:T(8,128)S(1)} collective-permute-done((f32[120,128]{1,0:T(8,128)S(1)}, f32[120,128]{1,0:T(8,128)S(1)}, u32[]{:S(2)}, u32[]{:S(2)}) %collective-permute-start.4) | collective-permute-done | bytes 61472 | tf_op jit(solution)/shard_map/ppermute | solution.py:484
  15.7 1.5 %collective-permute-done.5 = f32[120,128]{1,0:T(8,128)S(1)} collective-permute-done((f32[120,128]{1,0:T(8,128)S(1)}, f32[120,128]{1,0:T(8,128)S(1)}, u32[]{:S(2)}, u32[]{:S(2)}) %collective-permute-start.5) | collective-permute-done | bytes 61472 | tf_op jit(solution)/shard_map/ppermute | solution.py:485
  17.2 0.0 copy-start.3
  17.2 0.7 %collective-permute-start.6 = (f32[368,128]{1,0:T(8,128)S(1)}, f32[368,128]{1,0:T(8,128)S(1)}, u32[]{:S(2)}, u32[]{:S(2)}) collective-permute-start(f32[368,128]{1,0:T(8,128)S(1)} %constant_dynamic-update-slice_fusion.refs_4_), channel_id=1, source_target_pairs={{0,16},{16,0},{1,17},{17,1},{2,18},{18,2},{3,19},{19,3},{4,20},{20... | collective-permute-start | bytes 565256 | tf_op jit(solution)/shard_map/ppermute | solution.py:474
  17.9 5.0 %collective-permute-done.1.refs_3_ = s32[2,4,64,128]{3,2,1,0:T(8,128)S(1)} collective-permute-done((s32[2,4,64,128]{3,2,1,0:T(8,128)}, s32[2,4,64,128]{3,2,1,0:T(8,128)S(1)}, u32[]{:S(2)}, u32[]{:S(2)}) %collective-permute-start.1) | collective-permute-done | bytes 262176 | tf_op jit(solution)/shard_map/ppermute | solution.py:474
  22.9 0.0 copy-start.2
  22.9 3.9 %collective-permute-done.6.refs_5_ = f32[368,128]{1,0:T(8,128)S(1)} collective-permute-done((f32[368,128]{1,0:T(8,128)S(1)}, f32[368,128]{1,0:T(8,128)S(1)}, u32[]{:S(2)}, u32[]{:S(2)}) %collective-permute-start.6) | collective-permute-done | bytes 188448 | tf_op jit(solution)/shard_map/ppermute | solution.py:474
  26.8 0.0 copy-start.4
  26.8 0.0 collective-permute-done.refs_1_
  26.8 0.0 copy-done.3
  26.8 0.0 copy-done.2
  26.8 0.6 %copy-done.4 = f32[368,128]{1,0:T(8,128)} copy-done((f32[368,128]{1,0:T(8,128)}, f32[368,128]{1,0:T(8,128)S(1)}, u32[]{:S(2)}) %copy-start.4) | copy-done | bytes 188440
  27.5 0.0 copy-start.1
  27.5 0.8 %copy-done.1 = f32[4,4,64,128]{3,2,1,0:T(8,128)} copy-done((f32[4,4,64,128]{3,2,1,0:T(8,128)}, f32[4,4,64,128]{3,2,1,0:T(8,128)S(1)}, u32[]{:S(2)}) %copy-start.1) | copy-done | bytes 524312
  28.3 31.8 %local.1 = f32[4,4,64,128]{3,2,1,0:T(8,128)} custom-call(f32[4,4,64,128]{3,2,1,0:T(8,128)} %refs_0_.1, f32[4,4,64,128]{3,2,1,0:T(8,128)} %copy-done.1, s32[2,4,64,128]{3,2,1,0:T(8,128)} %get-tuple-element.10.refs_2_, s32[2,4,64,128]{3,2,1,0:T(8,128)} %copy-done.2, f32[368,128]{1,0:T(8,128)} %copy-done.3, f32[368,128]{1,0:T(8,128)} %copy-done.4), custom_call_target="tpu_custom_call" | custom-call | tf_op jit(solution)/shard_map/local/pallas_call | solution.py:455
  (7 shorter events, 0.0 us)
Async XLA Ops:
  0.0 2.9 %copy-start = (f32[4,4,64,128]{3,2,1,0:T(8,128)S(1)}, f32[4,4,64,128]{3,2,1,0:T(8,128)}, u32[]{:S(2)}) copy-start(f32[4,4,64,128]{3,2,1,0:T(8,128)} %refs_0_.1) | copy-start | bytes 1572868
  2.4 4.7 %collective-permute-start.2 = (f32[64,128]{1,0:T(8,128)}, f32[64,128]{1,0:T(8,128)S(1)}, u32[]{:S(2)}, u32[]{:S(2)}) collective-permute-start(f32[64,128]{1,0:T(8,128)} %get-tuple-element.11), channel_id=1, source_target_pairs={{0,1},{1,2},{2,3},{3,0},{4,5},{5,6},{6,7},{7,4},{8,9},{9,10},{10,1... | collective-permute-start | bytes 98312 | tf_op jit(solution)/shard_map/ppermute | solution.py:480
  2.9 23.9 %collective-permute-start = (f32[4,4,64,128]{3,2,1,0:T(8,128)S(1)}, f32[4,4,64,128]{3,2,1,0:T(8,128)S(1)}, u32[]{:S(2)}, u32[]{:S(2)}) collective-permute-start(f32[4,4,64,128]{3,2,1,0:T(8,128)S(1)} %copy-done), channel_id=1, source_target_pairs={{0,16},{16,0},{1,17},{17,1},{2,18},{18,2},{3,19},{19,3},{4,20},{20... | collective-permute-start | bytes 1572872 | tf_op jit(solution)/shard_map/ppermute | solution.py:474
  5.5 3.3 %collective-permute-start.3 = (f32[64,128]{1,0:T(8,128)}, f32[64,128]{1,0:T(8,128)S(1)}, u32[]{:S(2)}, u32[]{:S(2)}) collective-permute-start(f32[64,128]{1,0:T(8,128)} %get-tuple-element.12), channel_id=1, source_target_pairs={{0,3},{1,0},{2,1},{3,2},{4,7},{5,4},{6,5},{7,6},{8,11},{9,8},{10,9... | collective-permute-start | bytes 98312 | tf_op jit(solution)/shard_map/ppermute | solution.py:481
  6.8 16.0 %collective-permute-start.1 = (s32[2,4,64,128]{3,2,1,0:T(8,128)}, s32[2,4,64,128]{3,2,1,0:T(8,128)S(1)}, u32[]{:S(2)}, u32[]{:S(2)}) collective-permute-start(s32[2,4,64,128]{3,2,1,0:T(8,128)} %get-tuple-element.10.refs_2_), channel_id=1, source_target_pairs={{0,16},{16,0},{1,17},{17,1},{2,18},{18,2},{3,19},{19,3},{4,20},{20... | collective-permute-start | bytes 786440 | tf_op jit(solution)/shard_map/ppermute | solution.py:474
  8.8 2.4 %copy-start.5 = (f32[112,128]{1,0:T(8,128)S(1)}, f32[112,128]{1,0:T(8,128)}, u32[]{:S(2)}) copy-start(f32[112,128]{1,0:T(8,128)} %get-tuple-element.14) | copy-start | bytes 172036
  9.6 6.1 %collective-permute-start.4 = (f32[120,128]{1,0:T(8,128)S(1)}, f32[120,128]{1,0:T(8,128)S(1)}, u32[]{:S(2)}, u32[]{:S(2)}) collective-permute-start(f32[120,128]{1,0:T(8,128)S(1)} %pad_maximum_fusion), channel_id=1, source_target_pairs={{0,4},{4,8},{8,12},{12,0},{1,5},{5,9},{9,13},{13,1},{2,6},{6,10},{... | collective-permute-start | bytes 184328 | tf_op jit(solution)/shard_map/ppermute | solution.py:484
  11.2 6.0 %collective-permute-start.5 = (f32[120,128]{1,0:T(8,128)S(1)}, f32[120,128]{1,0:T(8,128)S(1)}, u32[]{:S(2)}, u32[]{:S(2)}) collective-permute-start(f32[120,128]{1,0:T(8,128)S(1)} %pad_maximum_fusion.1), channel_id=1, source_target_pairs={{0,12},{4,0},{8,4},{12,8},{1,13},{5,1},{9,5},{13,9},{2,14},{6,2},{... | collective-permute-start | bytes 184328 | tf_op jit(solution)/shard_map/ppermute | solution.py:485
  17.2 9.6 %copy-start.3 = (f32[368,128]{1,0:T(8,128)}, f32[368,128]{1,0:T(8,128)S(1)}, u32[]{:S(2)}) copy-start(f32[368,128]{1,0:T(8,128)S(1)} %constant_dynamic-update-slice_fusion.refs_4_) | copy-start | bytes 565252
  17.2 9.6 %collective-permute-start.6 = (f32[368,128]{1,0:T(8,128)S(1)}, f32[368,128]{1,0:T(8,128)S(1)}, u32[]{:S(2)}, u32[]{:S(2)}) collective-permute-start(f32[368,128]{1,0:T(8,128)S(1)} %constant_dynamic-update-slice_fusion.refs_4_), channel_id=1, source_target_pairs={{0,16},{16,0},{1,17},{17,1},{2,18},{18,2},{3,19},{19,3},{4,20},{20... | collective-permute-start | bytes 565256 | tf_op jit(solution)/shard_map/ppermute | solution.py:474
  22.9 3.9 %copy-start.2 = (s32[2,4,64,128]{3,2,1,0:T(8,128)}, s32[2,4,64,128]{3,2,1,0:T(8,128)S(1)}, u32[]{:S(2)}) copy-start(s32[2,4,64,128]{3,2,1,0:T(8,128)S(1)} %collective-permute-done.1.refs_3_) | copy-start | bytes 786436
  26.8 0.7 %copy-start.4 = (f32[368,128]{1,0:T(8,128)}, f32[368,128]{1,0:T(8,128)S(1)}, u32[]{:S(2)}) copy-start(f32[368,128]{1,0:T(8,128)S(1)} %collective-permute-done.6.refs_5_) | copy-start | bytes 565252
  27.5 0.8 %copy-start.1 = (f32[4,4,64,128]{3,2,1,0:T(8,128)}, f32[4,4,64,128]{3,2,1,0:T(8,128)S(1)}, u32[]{:S(2)}) copy-start(f32[4,4,64,128]{3,2,1,0:T(8,128)S(1)} %collective-permute-done.refs_1_) | copy-start | bytes 1572868

commit v2 on v1

--- a/solution.py
+++ b/solution.py
@@ -7,6 +7,7 @@
 from jax.experimental.pallas import tpu as pltpu
 from jax.sharding import PartitionSpec as P
 
+
 PASSES = 2
 HALO = 2 * PASSES
 LANES = 128
@@ -15,7 +16,11 @@
 LOW_BITS = 14
 
 VMEM = pl.BlockSpec(memory_space=pltpu.VMEM)
-PARAMS = pltpu.CompilerParams(vmem_limit_bytes=60 * 2**20)
+ANY = pl.BlockSpec(memory_space=pl.ANY)
+
+
+def params(mib):
+    return pltpu.CompilerParams(vmem_limit_bytes=mib * 2**20)
 
 
 def offsets():
@@ -42,7 +47,7 @@
 
 
 def pack_kernel(fields, code, flag, bits, ints, zlo, zhi, ylo, yhi):
-    count, sx, sy, sz = fields.shape
+    count, sx, sy, _ = fields.shape
     lane = lax.broadcasted_iota(jnp.int32, (sy, LANES), 1)
     low_side = jnp.zeros((sy, LANES), jnp.float32)
     high_side = jnp.zeros((sy, LANES), jnp.float32)
@@ -68,7 +73,7 @@
 
 def pack(fields, code, flag, bits):
     count, sx, sy, sz = fields.shape
-    rows = (count + 3) * sx * HALO
+    rows = (count + 3) * sx * HALO + 2 * HALO
     f32 = jnp.float32
     return pl.pallas_call(
         pack_kernel,
@@ -81,9 +86,49 @@
         ),
         in_specs=[VMEM] * 4,
         out_specs=(VMEM,) * 5,
-        compiler_params=PARAMS,
+        compiler_params=params(8),
         name="pack",
     )(fields, code, flag, bits)
+
+
+def corners_kernel(sy, low, high, ylo_in, yhi_in, ylo, yhi):
+    first = ylo.shape[0] - 2 * HALO
+    for side, column in enumerate((low, high)):
+        rows = pl.ds(first + side * HALO, HALO)
+        ylo[rows, :] = column[:HALO]
+        yhi[rows, :] = column[sy - HALO :]
+
+
+def add_corners(low, high, ylo, yhi):
+    shape = jax.ShapeDtypeStruct(ylo.shape, ylo.dtype)
+    return pl.pallas_call(
+        functools.partial(corners_kernel, low.shape[0]),
+        out_shape=(shape, shape),
+        in_specs=[VMEM] * 4,
+        out_specs=(VMEM, VMEM),
+        input_output_aliases={2: 0, 3: 1},
+        compiler_params=params(2),
+        name="corners",
+    )(low, high, ylo, yhi)
+
+
+def join_kernel(*refs):
+    out, row = refs[-1], 0
+    for ref in refs[:-1]:
+        out[pl.ds(row, ref.shape[0]), :] = ref[...]
+        row += ref.shape[0]
+
+
+def join(*pieces):
+    rows = sum(piece.shape[0] for piece in pieces)
+    return pl.pallas_call(
+        join_kernel,
+        out_shape=jax.ShapeDtypeStruct((rows, LANES), jnp.float32),
+        in_specs=[VMEM] * len(pieces),
+        out_specs=VMEM,
+        compiler_params=params(2),
+        name="join",
+    )(*pieces)
 
 
 class Box:
@@ -91,7 +136,7 @@
         self.count, self.sx, self.sy, self.blocks = count, sx, sy, blocks
         self.planes = sx * blocks
         self.tiles = -(-self.planes * GROUP // LANES)
-        self.rows = sy + 2 * TOP
+        self.rows = sy + 3 * TOP
         self.steps = -(-(sy + 2 * HALO) // 8)
 
     def near(self, reach):
@@ -103,7 +148,7 @@
     return lax.broadcasted_iota(jnp.int32, (8, LANES), 1)
 
 
-def fill(box, main_of, low_of, high_of, main, strip):
+def fill(box, main_of, low_of, high_of, strip):
     lane = lane_index()
 
     def step(t, _):
@@ -336,135 +381,174 @@
     lax.fori_loop(0, box.steps, step, 0)
 
 
-SCRATCH = ("mask", "smask", "inv", "sinv", "w", "sw", "hat", "shat", "icount", "scale", "sscale", "kappa", "skappa", "active", "sactive", "half", "shalf", "zbuf")
-
-
-def scratch_shapes(box):
-    p, k, r, n = box.planes, box.tiles, box.rows, box.count
-    f32 = jnp.float32
-    return [
-        pltpu.VMEM((26, p, r, LANES), f32),
-        pltpu.VMEM((26, k, r, LANES), f32),
-        pltpu.VMEM((p, r, LANES), f32),
-        pltpu.VMEM((k, r, LANES), f32),
-        pltpu.VMEM((n, p, r, LANES), f32),
-        pltpu.VMEM((n, k, r, LANES), f32),
-        pltpu.VMEM((n, 3, p, r, LANES), f32),
-        pltpu.VMEM((n, 9, k, r, LANES), f32),
-        pltpu.VMEM((p, r, LANES), f32),
-        pltpu.VMEM((p, r, LANES), f32),
-        pltpu.VMEM((k, r, LANES), f32),
-        pltpu.VMEM((p, r, LANES), f32),
-        pltpu.VMEM((k, r, LANES), f32),
-        pltpu.VMEM((p, r, LANES), jnp.int32),
-        pltpu.VMEM((k, r, LANES), jnp.int32),
-        pltpu.VMEM((2, p, r, LANES), f32),
-        pltpu.VMEM((2, k, r, LANES), f32),
-        pltpu.VMEM((2, box.blocks, r, LANES), f32),
-    ]
-
-
-def local_kernel(box, *refs):
-    nb, sx, sy, count = box.blocks, box.sx, box.sy, box.count
-    fields, refs = refs[:nb], refs[nb:]
-    ints, refs = refs[:nb], refs[nb:]
-    edges, refs = refs[:nb], refs[nb:]
-    out, refs = refs[0], dict(zip(SCRATCH, refs[1:]))
-    ymain = (count + 3) * sx * HALO
-    ylow, yhigh = 2 * sy, 2 * sy + ymain + 2 * HALO
-    own_rows, before, after = pl.ds(TOP, sy), pl.ds(TOP - HALO, HALO), pl.ds(TOP + sy, HALO)
-    zbuf = refs["zbuf"]
-    for b in range(nb):
-        for side in range(2):
-            zbuf[side, b, own_rows, :] = edges[b][pl.ds(side * sy, sy), :]
-            zbuf[side, b, before, :] = edges[b][pl.ds(ylow + ymain + side * HALO, HALO), :]
-            zbuf[side, b, after, :] = edges[b][pl.ds(yhigh + ymain + side * HALO, HALO), :]
-
-    def halo_rows(target, a, x):
-        b, p = divmod(x, sx)
-        row = (a * sx + p) * HALO
-        target[x, before, :] = edges[b][pl.ds(ylow + row, HALO), :]
-        target[x, after, :] = edges[b][pl.ds(yhigh + row, HALO), :]
-
-    def strips(a, main, strip):
+GEOMETRY = ("mask", "smask", "inv", "sinv", "icount", "scale", "sscale", "kappa", "skappa")
+
+
+def geometry_shapes(box):
+    p, k, r = box.planes, box.tiles, box.rows
+    shapes = [(26, p), (26, k), (p,), (k,), (p,), (p,), (k,), (p,), (k,)]
+    return [pltpu.VMEM((*shape, r, LANES), jnp.float32) for shape in shapes]
+
+
+class Edges:
+    def __init__(self, box, edges, zbuf):
+        self.box, self.edges, self.zbuf = box, edges, zbuf
+        sy, main = box.sy, (box.count + 3) * box.sx * HALO
+        self.ylow, self.yhigh, self.corner = 2 * sy, 2 * sy + main + 2 * HALO, main
+        self.own, self.before, self.after = pl.ds(TOP, sy), pl.ds(TOP - HALO, HALO), pl.ds(TOP + sy, HALO)
+
+    def columns(self):
+        for b, edge in enumerate(self.edges):
+            for side in range(2):
+                corner = self.corner + side * HALO
+                self.zbuf[side, b, self.own, :] = edge[pl.ds(side * self.box.sy, self.box.sy), :]
+                self.zbuf[side, b, self.before, :] = edge[pl.ds(self.ylow + corner, HALO), :]
+                self.zbuf[side, b, self.after, :] = edge[pl.ds(self.yhigh + corner, HALO), :]
+
+    def rows(self, target, a, x):
+        b, p = divmod(x, self.box.sx)
+        row = (a * self.box.sx + p) * HALO
+        target[x, self.before, :] = self.edges[b][pl.ds(self.ylow + row, HALO), :]
+        target[x, self.after, :] = self.edges[b][pl.ds(self.yhigh + row, HALO), :]
+
+    def strips(self, a, main, strip):
         def side_of(side):
             def get(b, r):
-                tile = zbuf[side, b, pl.ds(r, 8), :]
-                return [(tile, (a * sx + p) * HALO) for p in range(sx)]
+                tile = self.zbuf[side, b, pl.ds(r, 8), :]
+                return [(tile, (a * self.box.sx + p) * HALO) for p in range(self.box.sx)]
 
             return get
 
-        fill(box, lambda x, r: main[x, pl.ds(r, 8), :], side_of(0), side_of(1), main, strip)
-
-    half, shalf = refs["half"], refs["shalf"]
+        fill(self.box, lambda x, r: main[x, pl.ds(r, 8), :], side_of(0), side_of(1), strip)
+
+
+def geometry_kernel(box, *refs):
+    nb = box.blocks
+    ints, edge_refs, refs = refs[:nb], refs[nb : 2 * nb], refs[2 * nb :]
+    out, refs = dict(zip(GEOMETRY, refs)), refs[len(GEOMETRY) :]
+    active, sactive, half, shalf, zbuf = refs
+    edges = Edges(box, edge_refs, zbuf)
+    edges.columns()
     for x in range(box.planes):
-        b, p = divmod(x, sx)
-        refs["kappa"][x, own_rows, :] = ints[b][0, p].astype(jnp.float32)
-        active = ints[b][1, p]
-        half[0, x, own_rows, :] = jnp.bitwise_and(active, 2**LOW_BITS - 1).astype(jnp.float32)
-        half[1, x, own_rows, :] = jnp.right_shift(active, LOW_BITS).astype(jnp.float32)
-        halo_rows(refs["kappa"], count, x)
-        halo_rows(half.at[0], count + 1, x)
-        halo_rows(half.at[1], count + 2, x)
-    strips(count, refs["kappa"], refs["skappa"])
+        b, p = divmod(x, box.sx)
+        out["kappa"][x, edges.own, :] = ints[b][0, p].astype(jnp.float32)
+        member = ints[b][1, p]
+        half[0, x, edges.own, :] = jnp.bitwise_and(member, 2**LOW_BITS - 1).astype(jnp.float32)
+        half[1, x, edges.own, :] = jnp.right_shift(member, LOW_BITS).astype(jnp.float32)
+        edges.rows(out["kappa"], box.count, x)
+        edges.rows(half.at[0], box.count + 1, x)
+        edges.rows(half.at[1], box.count + 2, x)
+    edges.strips(box.count, out["kappa"], out["skappa"])
     for i in range(2):
-        strips(count + 1 + i, half.at[i], shalf.at[i])
+        edges.strips(box.count + 1 + i, half.at[i], shalf.at[i])
 
     def convert(t, _):
         rows = pl.ds(t * 8 + TOP - HALO, 8)
-        for full, kappa, active, n in (
-            (half, refs["kappa"], refs["active"], box.planes),
-            (shalf, refs["skappa"], refs["sactive"], box.tiles),
+        for full, kappa, bits, n in (
+            (half, out["kappa"], active, box.planes),
+            (shalf, out["skappa"], sactive, box.tiles),
         ):
             for x in range(n):
                 kappa[x, rows, :] = kappa[x, rows, :] * 2.0**-20
-                active[x, rows, :] = full[0, x, rows, :].astype(jnp.int32) + full[1, x, rows, :].astype(jnp.int32) * 2**LOW_BITS
+                low, high = full[0, x, rows, :].astype(jnp.int32), full[1, x, rows, :].astype(jnp.int32)
+                bits[x, rows, :] = low + high * 2**LOW_BITS
         return 0
 
     lax.fori_loop(0, box.steps, convert, 0)
-    masks_stage(box, refs)
-    volume_stage(box, refs, box.near(HALO - 1))
-
-    for f in range(count):
-        w = refs["w"].at[f]
+    out.update(active=active, sactive=sactive)
+    masks_stage(box, out)
+    volume_stage(box, out, box.near(HALO - 1))
+
+
+def geometry(box, ints, edges):
+    p, k, r = box.planes, box.tiles, box.rows
+    f32 = jnp.float32
+    return pl.pallas_call(
+        functools.partial(geometry_kernel, box),
+        out_shape=geometry_shapes(box),
+        in_specs=[VMEM] * (2 * box.blocks),
+        out_specs=[VMEM] * len(GEOMETRY),
+        scratch_shapes=[
+            pltpu.VMEM((p, r, LANES), jnp.int32),
+            pltpu.VMEM((k, r, LANES), jnp.int32),
+            pltpu.VMEM((2, p, r, LANES), f32),
+            pltpu.VMEM((2, k, r, LANES), f32),
+            pltpu.VMEM((2, box.blocks, r, LANES), f32),
+        ],
+        compiler_params=params(20),
+        name="geometry",
+    )(*ints, *edges)
+
+
+WORK = ("w", "sw", "hat", "shat")
+
+
+def fields_kernel(box, group, aliased, *refs):
+    nb, n = box.blocks, len(group)
+    fields, edge_refs, refs = refs[:nb], refs[nb : 2 * nb], refs[2 * nb :]
+    known, refs = dict(zip(GEOMETRY, refs)), refs[len(GEOMETRY) + aliased :]
+    merged, refs = refs[0], refs[1:]
+    known.update(zip(WORK, refs))
+    zbuf, result, done = refs[len(WORK) :]
+    edges = Edges(box, edge_refs, zbuf)
+    edges.columns()
+    for i, f in enumerate(group):
+        w, sw = known["w"].at[i], known["sw"].at[i]
         for x in range(box.planes):
-            b, p = divmod(x, sx)
-            w[x, own_rows, :] = fields[b][f, p]
-            halo_rows(w, f, x)
-        strips(f, w, refs["sw"].at[f])
-
-        def weigh(t, _, f=f):
-            rows = pl.ds(t * 8 + TOP - HALO, 8)
+            b, p = divmod(x, box.sx)
+            w[x, edges.own, :] = fields[b][f if b == 0 else i, p]
+            edges.rows(w, f, x)
+        edges.strips(f, w, sw)
+
+    def weigh(t, _):
+        rows = pl.ds(t * 8 + TOP - HALO, 8)
+        for i in range(n):
             for x in range(box.planes):
-                refs["w"][f, x, rows, :] = refs["w"][f, x, rows, :] * refs["kappa"][x, rows, :]
+                known["w"][i, x, rows, :] = known["w"][i, x, rows, :] * known["kappa"][x, rows, :]
             for k in range(box.tiles):
-                refs["sw"][f, k, rows, :] = refs["sw"][f, k, rows, :] * refs["skappa"][k, rows, :]
-            return 0
-
-        lax.fori_loop(0, box.steps, weigh, 0)
-
-    for group in chunks(list(range(count)), 2):
-        for step in range(PASSES):
-            reach = HALO - 1 - 2 * step
-            scatter_stage(box, refs, group, box.near(reach))
-            gather_stage(box, refs, group, box.near(reach - 1), None if step < PASSES - 1 else out)
-
-
-def local(box, fields, ints, edges):
+                known["sw"][i, k, rows, :] = known["sw"][i, k, rows, :] * known["skappa"][k, rows, :]
+        return 0
+
+    lax.fori_loop(0, box.steps, weigh, 0)
+    inner = list(range(n))
+    for step in range(PASSES):
+        reach = HALO - 1 - 2 * step
+        scatter_stage(box, known, inner, box.near(reach))
+        gather_stage(box, known, inner, box.near(reach - 1), None if step < PASSES - 1 else result)
+    copy = pltpu.make_async_copy(result, merged.at[pl.ds(group[0], n)], done)
+    copy.start()
+    copy.wait()
+
+
+def merge(box, group, fields, edges, known, merged):
+    p, k, r, n = box.planes, box.tiles, box.rows, len(group)
+    f32 = jnp.float32
     shape = fields[0].shape
+    aliased = merged is not None
+    operands = [*fields, *edges, *known]
+    specs = [VMEM] * len(operands)
     return pl.pallas_call(
-        functools.partial(local_kernel, box),
-        out_shape=jax.ShapeDtypeStruct(shape, jnp.float32),
-        in_specs=[VMEM] * (3 * box.blocks),
-        out_specs=VMEM,
-        scratch_shapes=scratch_shapes(box),
-        compiler_params=PARAMS,
-        name="local",
-    )(*fields, *ints, *edges)
+        functools.partial(fields_kernel, box, group, aliased),
+        out_shape=jax.ShapeDtypeStruct(shape, f32),
+        in_specs=specs + [ANY] * aliased,
+        out_specs=ANY,
+        scratch_shapes=[
+            pltpu.VMEM((n, p, r, LANES), f32),
+            pltpu.VMEM((n, k, r, LANES), f32),
+            pltpu.VMEM((n, 3, p, r, LANES), f32),
+            pltpu.VMEM((n, 9, k, r, LANES), f32),
+            pltpu.VMEM((2, box.blocks, r, LANES), f32),
+            pltpu.VMEM((n, *shape[1:]), f32),
+            pltpu.SemaphoreType.DMA(()),
+        ],
+        input_output_aliases={len(operands): 0} if aliased else {},
+        compiler_params=params(16),
+        name="merge",
+    )(*operands, *([merged] if aliased else []))
 
 
 def body(fields, volume_code, cut_flag, member_bits):
-    count, sx, sy, sz = fields.shape
+    count, sx, sy, _ = fields.shape
     size = lax.axis_size("gx")
 
     def from_x(value):
@@ -475,18 +559,24 @@
         return [lax.ppermute(value, "gx", ring("gx", -1)), lax.ppermute(value, "gx", ring("gx", 1))]
 
     ints, zlo, zhi, ylo, yhi = pack(fields, volume_code, cut_flag, member_bits)
-    all_fields = [fields] + from_x(fields)
-    all_ints = [ints] + from_x(ints)
     low = lax.ppermute(zhi, "gz", ring("gz", 1))
     high = lax.ppermute(zlo, "gz", ring("gz", -1))
-    ylo = jnp.concatenate([ylo, low[:HALO], high[:HALO]])
-    yhi = jnp.concatenate([yhi, low[sy - HALO :], high[sy - HALO :]])
+    all_ints = [ints] + from_x(ints)
+    box = Box(count, sx, sy, len(all_ints))
+    groups = chunks(list(range(count)), 2)
+    shared = [from_x(fields[groups[0][0] : groups[0][-1] + 1])]
+    ylo, yhi = add_corners(low, high, ylo, yhi)
     before = lax.ppermute(yhi, "gy", ring("gy", 1))
     after = lax.ppermute(ylo, "gy", ring("gy", -1))
-    edge = jnp.concatenate([low, high, before, after])
+    edge = join(low, high, before, after)
     all_edges = [edge] + from_x(edge)
-    box = Box(count, sx, sy, len(all_fields))
-    return local(box, all_fields, all_ints, all_edges)
+    for group in groups[1:]:
+        shared.append(from_x(fields[group[0] : group[-1] + 1]))
+    known = geometry(box, all_ints, all_edges)
+    merged = None
+    for group, others in zip(groups, shared):
+        merged = merge(box, group, [fields] + others, all_edges, known, merged)
+    return merged
 
 
 def solution(mesh):

time: 60.7 us -> 61.3 us (level)
  Pallas kernels: 34.2 us -> 29.5 us
  local copies, waits for them, and re-layouts: 1.48 us -> 5.86 us
  starting transfers between devices: 9.33 us -> 11.3 us
  other arithmetic: 0.84 us -> 0 us
    unnamed x15 -> x10, local copies, waits for them, and re-layouts: 1.47 us -> 4.79 us
    pallas_call x1 -> x5, Pallas kernels: 31.8 us -> 29 us  [the longest x2 22.9 us: merge(): pl.pallas_call(functools.partial(fields_kernel, box, group, aliased), out...]
    ppermute x3 -> x4, waiting for transfers between devices: 8.89 us -> 11.6 us  [from_x(): return [lax.ppermute(value, 'gx', ring('gx', 1))]]
    pallas_call x1, Pallas kernels: 2.41 us -> 0.53 us  [pack(): pl.pallas_call(pack_kernel, out_shape=(jax.ShapeDtypeStruct((2, sx, sy, s...]
    ppermute x1, waiting for transfers between devices: 1.62 us -> 0.01 us  [body(): high = lax.ppermute(zlo, 'gz', ring('gz', -1))]
    ppermute x1, waiting for transfers between devices: 1.45 us -> 0.07 us  [body(): after = lax.ppermute(ylo, 'gy', ring('gy', -1))]
    ppermute x3 -> x4, starting transfers between devices: 3.57 us -> 4.9 us  [from_x(): return [lax.ppermute(value, 'gx', ring('gx', 1))]]
    slice x2 -> x1, local copies, waits for them, and re-layouts: 0.01 us -> 1.07 us  [body(): shared = [from_x(fields[groups[0][0]:groups[0][-1] + 1])]]
  transfers between devices with their start and end apart: 7 -> 8, of which waited for: 5 -> 3; matrix products, arithmetic and copies ran while one was open for 1% -> 2% of each run, Pallas kernels for 0% -> 29%
where the time goes in v2:
time: 61.3 us; the launch traced here: 61 us
  Pallas kernels  29.5 us (48%)
  waiting for transfers between devices  14.2 us (23%)
  starting transfers between devices  11.3 us (18%)
  local copies, waits for them, and re-layouts  5.86 us (10%)
    pallas_call x2, Pallas kernels, merge(): pl.pallas_call(functools.partial(fields_kernel, box, group, aliased), out...  22.9 us
    ppermute x4, waiting for transfers between devices, from_x(): return [lax.ppermute(value, 'gx', ring('gx', 1))]  11.6 us
    pallas_call x1, Pallas kernels, geometry(): pl.pallas_call(functools.partial(geometry_kernel, box), out_shape=geometr...  6.11 us
    ppermute x4, starting transfers between devices, from_x(): return [lax.ppermute(value, 'gx', ring('gx', 1))]  4.9 us
    unnamed x10, local copies, waits for them, and re-layouts  4.79 us
    ppermute x1, waiting for transfers between devices, body(): before = lax.ppermute(yhi, 'gy', ring('gy', 1))  2.56 us
    ppermute x1, starting transfers between devices, body(): after = lax.ppermute(ylo, 'gy', ring('gy', -1))  2.25 us
    ppermute x1, starting transfers between devices, body(): high = lax.ppermute(zlo, 'gz', ring('gz', -1))  2.01 us
  transfers between devices with their start and end apart: 8, of which 3 were waited for; matrix products, arithmetic and copies ran while one was open for 2% of the time, Pallas kernels for 29%

profile of v2, /device:TPU:0, one launch (start us, length us, event | category | flops | bytes accessed | tf_op | source)
XLA Modules:
  0.0 61.0 jit_solution(5872079320734358427)
XLA Ops:
  0.0 0.0 copy-start
  0.0 1.0 %copy-done = f32[4,4,64,128]{3,2,1,0:T(8,128)S(1)} copy-done((f32[4,4,64,128]{3,2,1,0:T(8,128)S(1)}, f32[4,4,64,128]{3,2,1,0:T(8,128)}, u32[]{:S(2)}) %copy-start) | copy-done | bytes 524312
  1.0 0.0 copy-start.2
  1.0 0.9 %copy-done.2 = s32[4,64,128]{2,1,0:T(8,128)S(1)} copy-done((s32[4,64,128]{2,1,0:T(8,128)S(1)}, s32[4,64,128]{2,1,0:T(8,128)}, u32[]{:S(2)}) %copy-start.2) | copy-done | bytes 131096
  1.9 0.0 copy-start.3
  1.9 0.9 %copy-done.3 = s32[4,64,128]{2,1,0:T(8,128)S(1)} copy-done((s32[4,64,128]{2,1,0:T(8,128)S(1)}, s32[4,64,128]{2,1,0:T(8,128)}, u32[]{:S(2)}) %copy-start.3) | copy-done | bytes 131096
  2.9 0.0 copy-start.4
  2.9 0.9 %copy-done.4 = s32[4,64,128]{2,1,0:T(8,128)S(1)} copy-done((s32[4,64,128]{2,1,0:T(8,128)S(1)}, s32[4,64,128]{2,1,0:T(8,128)}, u32[]{:S(2)}) %copy-start.4) | copy-done | bytes 131096
  3.8 0.5 pack.1
  4.3 0.5 collective-permute-start.1
  4.8 2.0 %collective-permute-start.2 = (f32[64,128]{1,0:T(8,128)S(1)}, f32[64,128]{1,0:T(8,128)S(1)}, u32[]{:S(2)}, u32[]{:S(2)}) collective-permute-start(f32[64,128]{1,0:T(8,128)S(1)} %get-tuple-element.22), channel_id=1, source_target_pairs={{0,3},{1,0},{2,1},{3,2},{4,7},{5,4},{6,5},{7,6},{8,11},{9,8},{10,9... | collective-permute-start | bytes 98312 | tf_op jit(solution)/shard_map/ppermute | solution.py:563
  6.8 2.2 %collective-permute-start.6 = (s32[2,4,64,128]{3,2,1,0:T(8,128)S(1)}, s32[2,4,64,128]{3,2,1,0:T(8,128)S(1)}, u32[]{:S(2)}, u32[]{:S(2)}) collective-permute-start(s32[2,4,64,128]{3,2,1,0:T(8,128)S(1)} %get-tuple-element.27.refs_0_), channel_id=1, source_target_pairs={{0,16},{16,0},{1,17},{17,1},{2,18},{18,2},{3,19},{19,3},{4,20},{20... | collective-permute-start | bytes 786440 | tf_op jit(solution)/shard_map/ppermute | solution.py:558
  9.1 1.1 %fusion = (f32[2,4,64,128]{3,2,1,0:T(8,128)S(1)}, f32[2,4,64,128]{3,2,1,0:T(8,128)S(1)}) fusion(f32[4,4,64,128]{3,2,1,0:T(8,128)} %refs_0_.3), kind=kLoop, calls=%fused_computation | loop fusion | bytes 1048576 | tf_op jit(solution)/shard_map/slice | solution.py:567
  10.1 0.1 collective-permute-start.7
  10.2 2.0 %collective-permute-start = (f32[2,4,64,128]{3,2,1,0:T(8,128)S(1)}, f32[2,4,64,128]{3,2,1,0:T(8,128)S(1)}, u32[]{:S(2)}, u32[]{:S(2)}) collective-permute-start(f32[2,4,64,128]{3,2,1,0:T(8,128)S(1)} %get-tuple-element.38), channel_id=1, source_target_pairs={{0,16},{16,0},{1,17},{17,1},{2,18},{18,2},{3,19},{19,3},{4,20},{20... | collective-permute-start | bytes 786440 | tf_op jit(solution)/shard_map/ppermute | solution.py:558
  12.2 0.0 collective-permute-done.1.low.refs_0_
  12.2 0.0 collective-permute-done.2.high.refs_1_
  12.2 1.6 %collective-permute-start.3 = (f32[120,128]{1,0:T(8,128)S(1)}, f32[120,128]{1,0:T(8,128)S(1)}, u32[]{:S(2)}, u32[]{:S(2)}) collective-permute-start(f32[120,128]{1,0:T(8,128)S(1)} %get-tuple-element.25), channel_id=1, source_target_pairs={{0,4},{4,8},{8,12},{12,0},{1,5},{5,9},{9,13},{13,1},{2,6},{6,10},{... | collective-permute-start | bytes 184328 | tf_op jit(solution)/shard_map/ppermute | solution.py:569
  13.9 2.2 %collective-permute-start.4 = (f32[120,128]{1,0:T(8,128)S(1)}, f32[120,128]{1,0:T(8,128)S(1)}, u32[]{:S(2)}, u32[]{:S(2)}) collective-permute-start(f32[120,128]{1,0:T(8,128)S(1)} %get-tuple-element.26), channel_id=1, source_target_pairs={{0,12},{4,0},{8,4},{12,8},{1,13},{5,1},{9,5},{13,9},{2,14},{6,2},{... | collective-permute-start | bytes 184328 | tf_op jit(solution)/shard_map/ppermute | solution.py:570
  16.1 2.6 %collective-permute-done.3.refs_2_ = f32[120,128]{1,0:T(8,128)S(1)} collective-permute-done((f32[120,128]{1,0:T(8,128)S(1)}, f32[120,128]{1,0:T(8,128)S(1)}, u32[]{:S(2)}, u32[]{:S(2)}) %collective-permute-start.3) | collective-permute-done | bytes 61472 | tf_op jit(solution)/shard_map/ppermute | solution.py:569
  18.7 0.1 collective-permute-done.4.refs_3_
  18.8 0.6 collective-permute-start.5
  19.4 0.0 collective-permute-done.6.refs_1_
  19.4 11.6 %collective-permute-done.5.refs_3_ = f32[368,128]{1,0:T(8,128)S(1)} collective-permute-done((f32[368,128]{1,0:T(8,128)S(1)}, f32[368,128]{1,0:T(8,128)S(1)}, u32[]{:S(2)}, u32[]{:S(2)}) %collective-permute-start.5) | collective-permute-done | bytes 188448 | tf_op jit(solution)/shard_map/ppermute | solution.py:558
  30.9 6.1 %geometry.1 = (f32[26,8,88,128]{3,2,1,0:T(8,128)S(1)}, f32[26,1,88,128]{3,2,1,0:T(8,128)S(1)}, f32[8,88,128]{2,1,0:T(8,128)S(1)}, f32[1,88,128]{2,1,0:T(8,128)S(...) custom-call(s32[2,4,64,128]{3,2,1,0:T(8,128)S(1)} %get-tuple-element, ...), custom_call_target="tpu_custom_call" | custom-call | tf_op jit(solution)/shard_map/geometry/pallas_call | solution.py:466
  37.1 0.0 collective-permute-done.7.refs_1_
  37.1 0.0 copy-start.1
  37.1 1.0 %copy-done.1 = f32[4,4,64,128]{3,2,1,0:T(8,128)S(1)} copy-done((f32[4,4,64,128]{3,2,1,0:T(8,128)S(1)}, f32[4,4,64,128]{3,2,1,0:T(8,128)}, u32[]{:S(2)}) %copy-start.1) | copy-done | bytes 524312
  38.1 11.4 %merge.2.refs_13_ = f32[4,4,64,128]{3,2,1,0:T(8,128)} custom-call(f32[4,4,64,128]{3,2,1,0:T(8,128)S(1)} %copy-done.1, f32[2,4,64,128]{3,2,1,0:T(8,128)S(1)} %collective-permute-done.7.refs_1_, f32[368,128]{1,0:T(8,128)S(1)} %join.1.refs_2_, f32[368,128]{1,0:T(8,128)S(1)} %collective-permute-done.5.refs_3_, f32[26,8,88,128]{3,2,1,0:T(8,128)S(1)} %get-tuple-element.28.refs_4_, ...), custom_call_target="tpu_custom_call" | custom-call | tf_op jit(solution)/shard_map/merge/pallas_call | solution.py:530
  49.6 0.0 collective-permute-done.refs_1_
  49.6 11.4 %merge.3 = f32[4,4,64,128]{3,2,1,0:T(8,128)} custom-call(f32[4,4,64,128]{3,2,1,0:T(8,128)S(1)} %copy-done.1, f32[2,4,64,128]{3,2,1,0:T(8,128)S(1)} %collective-permute-done.refs_1_, f32[368,128]{1,0:T(8,128)S(1)} %join.1.refs_2_, f32[368,128]{1,0:T(8,128)S(1)} %collective-permute-done.5.refs_3_, ...), custom_call_target="tpu_custom_call", output_to_operand_aliasing={{}: (13, {})} | custom-call | tf_op jit(solution)/shard_map/merge/pallas_call | solution.py:530
  (2 shorter events, 0.0 us)
Async XLA Ops:
  0.0 1.0 %copy-start = (f32[4,4,64,128]{3,2,1,0:T(8,128)S(1)}, f32[4,4,64,128]{3,2,1,0:T(8,128)}, u32[]{:S(2)}) copy-start(f32[4,4,64,128]{3,2,1,0:T(8,128)} %refs_0_.3) | copy-start | bytes 1572868
  1.0 0.9 %copy-start.2 = (s32[4,64,128]{2,1,0:T(8,128)S(1)}, s32[4,64,128]{2,1,0:T(8,128)}, u32[]{:S(2)}) copy-start(s32[4,64,128]{2,1,0:T(8,128)} %code.1) | copy-start | bytes 393220
  1.9 0.9 %copy-start.3 = (s32[4,64,128]{2,1,0:T(8,128)S(1)}, s32[4,64,128]{2,1,0:T(8,128)}, u32[]{:S(2)}) copy-start(s32[4,64,128]{2,1,0:T(8,128)} %flag.1) | copy-start | bytes 393220
  2.9 0.9 %copy-start.4 = (s32[4,64,128]{2,1,0:T(8,128)S(1)}, s32[4,64,128]{2,1,0:T(8,128)}, u32[]{:S(2)}) copy-start(s32[4,64,128]{2,1,0:T(8,128)} %bits.1) | copy-start | bytes 393220
  4.3 7.9 %collective-permute-start.1 = (f32[64,128]{1,0:T(8,128)S(1)}, f32[64,128]{1,0:T(8,128)S(1)}, u32[]{:S(2)}, u32[]{:S(2)}) collective-permute-start(f32[64,128]{1,0:T(8,128)S(1)} %get-tuple-element.21), channel_id=1, source_target_pairs={{0,1},{1,2},{2,3},{3,0},{4,5},{5,6},{6,7},{7,4},{8,9},{9,10},{10,1... | collective-permute-start | bytes 98312 | tf_op jit(solution)/shard_map/ppermute | solution.py:562
  4.8 7.4 %collective-permute-start.2 = (f32[64,128]{1,0:T(8,128)S(1)}, f32[64,128]{1,0:T(8,128)S(1)}, u32[]{:S(2)}, u32[]{:S(2)}) collective-permute-start(f32[64,128]{1,0:T(8,128)S(1)} %get-tuple-element.22), channel_id=1, source_target_pairs={{0,3},{1,0},{2,1},{3,2},{4,7},{5,4},{6,5},{7,6},{8,11},{9,8},{10,9... | collective-permute-start | bytes 98312 | tf_op jit(solution)/shard_map/ppermute | solution.py:563
  6.8 12.5 %collective-permute-start.6 = (s32[2,4,64,128]{3,2,1,0:T(8,128)S(1)}, s32[2,4,64,128]{3,2,1,0:T(8,128)S(1)}, u32[]{:S(2)}, u32[]{:S(2)}) collective-permute-start(s32[2,4,64,128]{3,2,1,0:T(8,128)S(1)} %get-tuple-element.27.refs_0_), channel_id=1, source_target_pairs={{0,16},{16,0},{1,17},{17,1},{2,18},{18,2},{3,19},{19,3},{4,20},{20... | collective-permute-start | bytes 786440 | tf_op jit(solution)/shard_map/ppermute | solution.py:558
  10.1 26.9 %collective-permute-start.7 = (f32[2,4,64,128]{3,2,1,0:T(8,128)S(1)}, f32[2,4,64,128]{3,2,1,0:T(8,128)S(1)}, u32[]{:S(2)}, u32[]{:S(2)}) collective-permute-start(f32[2,4,64,128]{3,2,1,0:T(8,128)S(1)} %get-tuple-element.37), channel_id=1, source_target_pairs={{0,16},{16,0},{1,17},{17,1},{2,18},{18,2},{3,19},{19,3},{4,20},{20... | collective-permute-start | bytes 786440 | tf_op jit(solution)/shard_map/ppermute | solution.py:558
  10.2 39.3 %collective-permute-start = (f32[2,4,64,128]{3,2,1,0:T(8,128)S(1)}, f32[2,4,64,128]{3,2,1,0:T(8,128)S(1)}, u32[]{:S(2)}, u32[]{:S(2)}) collective-permute-start(f32[2,4,64,128]{3,2,1,0:T(8,128)S(1)} %get-tuple-element.38), channel_id=1, source_target_pairs={{0,16},{16,0},{1,17},{17,1},{2,18},{18,2},{3,19},{19,3},{4,20},{20... | collective-permute-start | bytes 786440 | tf_op jit(solution)/shard_map/ppermute | solution.py:558
  12.2 6.4 %collective-permute-start.3 = (f32[120,128]{1,0:T(8,128)S(1)}, f32[120,128]{1,0:T(8,128)S(1)}, u32[]{:S(2)}, u32[]{:S(2)}) collective-permute-start(f32[120,128]{1,0:T(8,128)S(1)} %get-tuple-element.25), channel_id=1, source_target_pairs={{0,4},{4,8},{8,12},{12,0},{1,5},{5,9},{9,13},{13,1},{2,6},{6,10},{... | collective-permute-start | bytes 184328 | tf_op jit(solution)/shard_map/ppermute | solution.py:569
  13.9 4.9 %collective-permute-start.4 = (f32[120,128]{1,0:T(8,128)S(1)}, f32[120,128]{1,0:T(8,128)S(1)}, u32[]{:S(2)}, u32[]{:S(2)}) collective-permute-start(f32[120,128]{1,0:T(8,128)S(1)} %get-tuple-element.26), channel_id=1, source_target_pairs={{0,12},{4,0},{8,4},{12,8},{1,13},{5,1},{9,5},{13,9},{2,14},{6,2},{... | collective-permute-start | bytes 184328 | tf_op jit(solution)/shard_map/ppermute | solution.py:570
  18.8 12.2 %collective-permute-start.5 = (f32[368,128]{1,0:T(8,128)S(1)}, f32[368,128]{1,0:T(8,128)S(1)}, u32[]{:S(2)}, u32[]{:S(2)}) collective-permute-start(f32[368,128]{1,0:T(8,128)S(1)} %join.1.refs_2_), channel_id=1, source_target_pairs={{0,16},{16,0},{1,17},{17,1},{2,18},{18,2},{3,19},{19,3},{4,20},{20... | collective-permute-start | bytes 565256 | tf_op jit(solution)/shard_map/ppermute | solution.py:558
  37.1 1.0 %copy-start.1 = (f32[4,4,64,128]{3,2,1,0:T(8,128)S(1)}, f32[4,4,64,128]{3,2,1,0:T(8,128)}, u32[]{:S(2)}) copy-start(f32[4,4,64,128]{3,2,1,0:T(8,128)} %refs_0_.3) | copy-start | bytes 1572868

commit v3 on v0

v3 whole, which is shorter than its diff:
```python
import functools

import jax
import jax.numpy as jnp
from jax import lax
from jax.experimental import pallas as pl
from jax.experimental.pallas import tpu as pltpu
from jax.sharding import PartitionSpec as P


PASSES = 2
HALO = 2 * PASSES
LANES = 128
GROUP = 16
TOP = 16
LOW_BITS = 14

VMEM = pl.BlockSpec(memory_space=pltpu.VMEM)
ANY = pl.BlockSpec(memory_space=pltpu.HBM)


def params(mib):
    return pltpu.CompilerParams(vmem_limit_bytes=int(mib * 2**20))


def offsets():
    return [(dx, dy, dz) for dx in (-1, 0, 1) for dy in (-1, 0, 1) for dz in (-1, 0, 1)]


def bit_of(dx, dy, dz):
    return 9 * (dx + 1) + 3 * (dy + 1) + (dz + 1)


def slot_of(dx, dy, dz):
    index = bit_of(dx, dy, dz)
    return index if index < 13 else index - 1


def roll(value, shift):
    shift = shift % LANES
    return value if shift == 0 else pltpu.roll(value, shift, 1)


def ring(axis, step):
    count = lax.axis_size(axis)
    return [(i, (i + step) % count) for i in range(count)]


def pack_kernel(fields, code, flag, bits, *refs):
    pairs, refs = refs[:-9], refs[-9:]
    ints, zlo, zhi, ylo, yhi, flag_v, bits_v, sems, field_sems = refs
    count, sx, sy, _ = fields.shape
    copies = [
        pltpu.make_async_copy(flag, flag_v, sems.at[0]),
        pltpu.make_async_copy(bits, bits_v, sems.at[1]),
        pltpu.make_async_copy(code, ints.at[0], sems.at[2]),
    ]
    loads, first = [], 0
    for i, pair in enumerate(pairs):
        loads.append(pltpu.make_async_copy(fields.at[pl.ds(first, pair.shape[0])], pair, field_sems.at[i]))
        first += pair.shape[0]
    for copy in copies + loads:
        copy.start()
    lane = lax.broadcasted_iota(jnp.int32, (sy, LANES), 1)
    sides = [jnp.zeros((sy, LANES), jnp.float32)] * 2

    def place(a, p, plane, sides):
        row = (a * sx + p) * HALO
        ylo[pl.ds(row, HALO), :] = plane[:HALO]
        yhi[pl.ds(row, HALO), :] = plane[sy - HALO :]
        here = (lane >= row) & (lane < row + HALO)
        return [
            jnp.where(here, roll(plane, row), sides[0]),
            jnp.where(here, roll(plane, row + HALO), sides[1]),
        ]

    for copy in copies:
        copy.wait()
    for p in range(sx):
        active = bits_v[p] * flag_v[p]
        ints[1, p] = active
        low = jnp.bitwise_and(active, 2**LOW_BITS - 1).astype(jnp.float32)
        high = jnp.right_shift(active, LOW_BITS).astype(jnp.float32)
        for i, plane in enumerate((ints[0, p].astype(jnp.float32), low, high)):
            sides = place(count + i, p, plane, sides)
    f = 0
    for pair, load in zip(pairs, loads):
        load.wait()
        for i in range(pair.shape[0]):
            for p in range(sx):
                sides = place(f, p, pair[i, p], sides)
            f += 1
    zlo[...], zhi[...] = sides


def pack(groups, fields, code, flag, bits):
    count, sx, sy, sz = fields.shape
    rows = (count + 3) * sx * HALO + 2 * HALO
    f32 = jnp.float32
    pairs = [pltpu.VMEM((len(group), sx, sy, sz), f32) for group in groups]
    outs = pl.pallas_call(
        pack_kernel,
        out_shape=(
            *pairs,
            pltpu.VMEM((2, sx, sy, sz), jnp.int32),
            pltpu.VMEM((sy, LANES), f32),
            pltpu.VMEM((sy, LANES), f32),
            pltpu.VMEM((rows, LANES), f32),
            pltpu.VMEM((rows, LANES), f32),
        ),
        in_specs=[ANY] * 4,
        out_specs=(VMEM,) * (len(pairs) + 5),
        scratch_shapes=[
            pltpu.VMEM((sx, sy, sz), jnp.int32),
            pltpu.VMEM((sx, sy, sz), jnp.int32),
            pltpu.SemaphoreType.DMA((3,)),
            pltpu.SemaphoreType.DMA((len(pairs),)),
        ],
        compiler_params=params(62.9),
        name="pack",
    )(fields, code, flag, bits)
    return outs[: len(pairs)], *outs[len(pairs) :]


def corners_kernel(sy, low, high, ylo_in, yhi_in, ylo, yhi):
    first = ylo.shape[0] - 2 * HALO
    for side, column in enumerate((low, high)):
        rows = pl.ds(first + side * HALO, HALO)
        ylo[rows, :] = column[:HALO]
        yhi[rows, :] = column[sy - HALO :]


def add_corners(low, high, ylo, yhi):
    shape = jax.ShapeDtypeStruct(ylo.shape, ylo.dtype)
    return pl.pallas_call(
        functools.partial(corners_kernel, low.shape[0]),
        out_shape=(shape, shape),
        in_specs=[VMEM] * 4,
        out_specs=(VMEM, VMEM),
        input_output_aliases={2: 0, 3: 1},
        compiler_params=params(2),
        name="corners",
    )(low, high, ylo, yhi)


def join_kernel(*refs):
    out, row = refs[-1], 0
    for ref in refs[:-1]:
        out[pl.ds(row, ref.shape[0]), :] = ref[...]
        row += ref.shape[0]


def join(*pieces):
    rows = sum(piece.shape[0] for piece in pieces)
    return pl.pallas_call(
        join_kernel,
        out_shape=jax.ShapeDtypeStruct((rows, LANES), jnp.float32),
        in_specs=[VMEM] * len(pieces),
        out_specs=VMEM,
        compiler_params=params(2),
        name="join",
    )(*pieces)


class Box:
    def __init__(self, count, sx, sy, blocks):
        self.count, self.sx, self.sy, self.blocks = count, sx, sy, blocks
        self.planes = sx * blocks
        self.tiles = -(-self.planes * GROUP // LANES)
        self.steps = -(-(sy + 2 * HALO) // 8)
        self.rows = TOP + sy + 8

    def near(self, reach):
        return sorted({x % self.planes for x in range(-reach, self.sx + reach)})

    def first(self, t):
        return t * 8 + TOP - HALO


def lane_index():
    return lax.broadcasted_iota(jnp.int32, (8, LANES), 1)


def roll_groups(values, shift):
    count = len(values)
    rolled = [roll(v, shift) for v in values]
    if count == 1 or shift == 0:
        return rolled
    lane = lane_index()
    if shift > 0:
        return [jnp.where(lane < shift, rolled[(k - 1) % count], rolled[k]) for k in range(count)]
    return [jnp.where(lane >= LANES + shift, rolled[(k + 1) % count], rolled[k]) for k in range(count)]


def add(left, right):
    return right if left is None else left + right


def from_strip(tiles, x, column, lane):
    tile, first = divmod(x * GROUP + column, LANES)
    return roll(tiles[tile], lane - first)


LAST = HALO - 1
NEXT = 3 * HALO


def version(dx, dz):
    return 3 * (dx + 1) + dz + 1


def spread_strip(box, tiles, target, r):
    for dx in (-1, 0, 1):
        for dz in (-1, 0, 1):
            shifted = roll_groups(tiles, -GROUP * dx - dz)
            for k in range(box.tiles):
                target[version(dx, dz), k, pl.ds(r, 8), :] = shifted[k]


def spread_plane(value, tiles, target, x, r):
    lane = lane_index()
    before, after = from_strip(tiles, x, LAST, 0), from_strip(tiles, x, NEXT, LANES - 1)
    target[0, x, pl.ds(r, 8), :] = jnp.where(lane == 0, before, roll(value, 1))
    target[2, x, pl.ds(r, 8), :] = jnp.where(lane == LANES - 1, after, roll(value, -1))


def center_strip(box, source, r):
    return [source[version(0, 0), k, pl.ds(r, 8), :] for k in range(box.tiles)]


def masked_strip(box, masks, sources, sign, r):
    sums = [[None] * box.tiles for _ in sources]
    for dx, dy, dz in offsets():
        for k in range(box.tiles):
            mask = None
            if (dx, dy, dz) != (0, 0, 0):
                mask = masks[slot_of(dx, dy, dz), k, pl.ds(r, 8), :]
            for f, source in enumerate(sources):
                piece = source[version(sign * dx, sign * dz), k, pl.ds(r + sign * dy, 8), :]
                sums[f][k] = add(sums[f][k], piece if mask is None else piece * mask)
    return sums


def masked_planes(box, masks, sources, sign, xs, r):
    sums = [{x: None for x in xs} for _ in sources]
    for dy in (-1, 0, 1):
        for dz in (-1, 0, 1):
            for at in range(box.planes):
                targets = [((at - sign * dx) % box.planes, dx) for dx in (-1, 0, 1)]
                targets = [(x, dx) for x, dx in targets if x in xs]
                if not targets:
                    continue
                cells = [source[sign * dz + 1, at, pl.ds(r + sign * dy, 8), :] for source in sources]
                for x, dx in targets:
                    mask = None
                    if (dx, dy, dz) != (0, 0, 0):
                        mask = masks[slot_of(dx, dy, dz), x, pl.ds(r, 8), :]
                    for f, cell in enumerate(cells):
                        sums[f][x] = add(sums[f][x], cell if mask is None else cell * mask)
    return sums


def stage(box, masks, smasks, scale, sscale, sources, ssources, targets, stargets, sign, xs):
    def spread(r):
        for target, starget in zip(targets, stargets):
            tiles = center_strip(box, starget, r)
            for x in xs:
                spread_plane(target[1, x, pl.ds(r, 8), :], tiles, target, x, r)

    def step(t, _):
        r = box.first(t)
        sums = masked_strip(box, smasks, ssources, sign, r)
        for f, starget in enumerate(stargets):
            tiles = [total * sscale[k, pl.ds(r, 8), :] for k, total in enumerate(sums[f])]
            spread_strip(box, tiles, starget, r)
        spread(r - 8)
        sums = masked_planes(box, masks, sources, sign, xs, r)
        for f, target in enumerate(targets):
            for x in xs:
                target[1, x, pl.ds(r, 8), :] = sums[f][x] * scale[x, pl.ds(r, 8), :]
        return 0

    lax.fori_loop(0, box.steps, step, 0)
    spread(box.first(box.steps - 1))


def bit_value(active, dx, dy, dz):
    return jnp.bitwise_and(jnp.right_shift(active, bit_of(dx, dy, dz)), 1).astype(jnp.float32)


GEOMETRY = ("own", "sown", "from", "sfrom", "inv", "sinv", "icount", "scale", "sscale", "kappa", "skappa")


def geometry_shapes(box):
    p, k, r = box.planes, box.tiles, box.rows
    shapes = [(26, p), (26, k), (26, p), (26, k), (p,), (k,), (p,), (p,), (k,), (p,), (k,)]
    return [pltpu.VMEM((*shape, r, LANES), jnp.float32) for shape in shapes]


class Edges:
    def __init__(self, box, edges):
        self.box, self.edges = box, edges
        sy, main = box.sy, (box.count + 3) * box.sx * HALO
        self.ylow, self.yhigh, self.corner = 2 * sy, 2 * sy + main + 2 * HALO, main
        self.own, self.before, self.after = pl.ds(TOP, sy), pl.ds(TOP - HALO, HALO), pl.ds(TOP + sy, HALO)

    def columns(self, zbuf):
        for b, edge in enumerate(self.edges):
            for side in range(2):
                corner = self.corner + side * HALO
                zbuf[side, b, self.own, :] = edge[pl.ds(side * self.box.sy, self.box.sy), :]
                zbuf[side, b, self.before, :] = edge[pl.ds(self.ylow + corner, HALO), :]
                zbuf[side, b, self.after, :] = edge[pl.ds(self.yhigh + corner, HALO), :]

    def row(self, a, x):
        return (a * self.box.sx + x % self.box.sx) * HALO

    def rows(self, a, x):
        edge = self.edges[x // self.box.sx]
        row = self.row(a, x)
        return edge[pl.ds(self.ylow + row, HALO), :], edge[pl.ds(self.yhigh + row, HALO), :]

    def strip(self, main, low_of, high_of, a, r):
        lane = lane_index()
        out = [None] * self.box.tiles
        for b in range(self.box.blocks):
            low, high = low_of(b, r), high_of(b, r)
            for p in range(self.box.sx):
                x = b * self.box.sx + p
                tile, first = divmod(x * GROUP, LANES)
                plane = main[x, pl.ds(r, 8), :]
                column = self.row(a, x)
                for c, (data, at) in enumerate(((low, column), (plane, 0), (plane, LANES - HALO), (high, column))):
                    to = first + c * HALO
                    moved = roll(data, to - at)
                    out[tile] = moved if out[tile] is None else jnp.where(lane >= to, moved, out[tile])
        return out


def geometry_kernel(box, *refs):
    nb = box.blocks
    ints, edge_refs, refs = refs[:nb], refs[nb : 2 * nb], refs[2 * nb :]
    out, refs = dict(zip(GEOMETRY, refs)), refs[len(GEOMETRY) :]
    active, sactive, kappa, skappa, zbuf = refs
    edges = Edges(box, edge_refs)
    edges.columns(zbuf)
    unit = 2.0**-20

    def whole(low, high):
        return low.astype(jnp.int32) + high.astype(jnp.int32) * 2**LOW_BITS

    for x in range(box.planes):
        b, p = divmod(x, box.sx)
        kappa[1, x, edges.own, :] = ints[b][0, p].astype(jnp.float32) * unit
        active[1, x, edges.own, :] = ints[b][1, p]
        for here, rows in enumerate((edges.before, edges.after)):
            code, low, high = [edges.rows(box.count + i, x)[here] for i in range(3)]
            kappa[1, x, rows, :] = code * unit
            active[1, x, rows, :] = whole(low, high)

    def code_of(side):
        return lambda b, r: zbuf[side, b, pl.ds(r, 8), :] * unit

    def bits_of(side):
        def get(b, r):
            tile = zbuf[side, b, pl.ds(r, 8), :]
            return whole(tile, roll(tile, -box.sx * HALO))

        return get

    for t in range(box.steps):
        r = box.first(t)
        for main, strip, halo, a in ((kappa, skappa, code_of, box.count), (active, sactive, bits_of, box.count + 1)):
            tiles = edges.strip(main.at[1], halo(0), halo(1), a, r)
            spread_strip(box, tiles, strip, r)

    def spread(t, _):
        r = box.first(t)
        for main, strip in ((kappa, skappa), (active, sactive)):
            tiles = center_strip(box, strip, r)
            for x in range(box.planes):
                spread_plane(main[1, x, pl.ds(r, 8), :], tiles, main, x, r)
        return 0

    lax.fori_loop(0, box.steps, spread, 0, unroll=3)

    def masks(t, _):
        r = box.first(t)
        rows = pl.ds(r, 8)
        for n, center, source, values, own, back, icount, scale, plain in (
            (box.planes, 1, active, kappa, "own", "from", "icount", "scale", "kappa"),
            (box.tiles, version(0, 0), sactive, skappa, "sown", "sfrom", None, "sscale", "skappa"),
        ):
            for x in range(n):
                here, total = source[center, x, rows, :], None
                for dx, dy, dz in offsets():
                    if (dx, dy, dz) == (0, 0, 0):
                        continue
                    bit = bit_value(here, dx, dy, dz)
                    out[own][slot_of(dx, dy, dz), x, rows, :] = bit
                    total = add(total, bit)
                    if center == 1:
                        there = source[1 - dz, (x - dx) % box.planes, pl.ds(r - dy, 8), :]
                    else:
                        there = source[version(-dx, -dz), x, pl.ds(r - dy, 8), :]
                    out[back][slot_of(dx, dy, dz), x, rows, :] = bit_value(there, dx, dy, dz)
                inverse = 1.0 / (total + 1.0)
                value = values[center, x, rows, :]
                out[plain][x, rows, :] = value
                out[scale][x, rows, :] = inverse * value
                if icount is not None:
                    out[icount][x, rows, :] = inverse
        return 0

    lax.fori_loop(0, box.steps, masks, 0)

    def volumes(t, _):
        r = box.first(t)
        totals = masked_strip(box, out["sfrom"], [skappa], -1, r)[0]
        for k, total in enumerate(totals):
            out["sinv"][k, pl.ds(r, 8), :] = 1.0 / total
        totals = masked_planes(box, out["from"], [kappa], -1, box.near(HALO - 1), r)[0]
        for x, total in totals.items():
            out["inv"][x, pl.ds(r, 8), :] = 1.0 / total
        return 0

    lax.fori_loop(0, box.steps, volumes, 0)


def geometry(box, ints, edges):
    p, k, r = box.planes, box.tiles, box.rows
    f32 = jnp.float32
    return pl.pallas_call(
        functools.partial(geometry_kernel, box),
        out_shape=geometry_shapes(box),
        in_specs=[VMEM] * (2 * box.blocks),
        out_specs=[VMEM] * len(GEOMETRY),
        scratch_shapes=[
            pltpu.VMEM((3, p, r, LANES), jnp.int32),
            pltpu.VMEM((9, k, r, LANES), jnp.int32),
            pltpu.VMEM((3, p, r, LANES), f32),
            pltpu.VMEM((9, k, r, LANES), f32),
            pltpu.VMEM((2, box.blocks, r, LANES), f32),
        ],
        compiler_params=params(8),
        name="geometry",
    )(*ints, *edges)


def fields_kernel(box, group, aliased, *refs):
    nb, n = box.blocks, len(group)
    fields, edge_refs, refs = refs[:nb], refs[nb : 2 * nb], refs[2 * nb :]
    known, refs = dict(zip(GEOMETRY, refs)), refs[len(GEOMETRY) + aliased :]
    merged, w, sw, hat, shat, zbuf, result, done = refs
    edges = Edges(box, edge_refs)
    edges.columns(zbuf)
    for i, f in enumerate(group):
        for x in range(box.planes):
            b, p = divmod(x, box.sx)
            before, after = edges.rows(f, x)
            w[i, 1, x, edges.own, :] = fields[b][i, p]
            w[i, 1, x, edges.before, :] = before
            w[i, 1, x, edges.after, :] = after

    def halo(side):
        return lambda b, r: zbuf[side, b, pl.ds(r, 8), :]

    def weigh(t, _):
        rows = pl.ds(box.first(t), 8)
        for i, f in enumerate(group):
            tiles = edges.strip(w.at[i, 1], halo(0), halo(1), f, box.first(t))
            tiles = [tile * known["skappa"][k, rows, :] for k, tile in enumerate(tiles)]
            spread_strip(box, tiles, sw.at[i], box.first(t))
            for x in range(box.planes):
                value = w[i, 1, x, rows, :] * known["kappa"][x, rows, :]
                w[i, 1, x, rows, :] = value
                spread_plane(value, tiles, w.at[i], x, box.first(t))
        return 0

    lax.fori_loop(0, box.steps, weigh, 0, unroll=3)

    def each(ref):
        return [ref.at[i] for i in range(n)]

    copy = pltpu.make_async_copy(result, merged.at[pl.ds(group[0], n)], done)
    for step in range(PASSES):
        reach = HALO - 1 - 2 * step
        stage(box, known["from"], known["sfrom"], known["inv"], known["sinv"], each(w), each(sw), each(hat), each(shat), -1, box.near(reach))
        if step < PASSES - 1:
            stage(box, known["own"], known["sown"], known["scale"], known["sscale"], each(hat), each(shat), each(w), each(sw), 1, box.near(reach - 1))

    def last(t, _):
        r = TOP + t * 8
        sums = masked_planes(box, known["own"], each(hat), 1, box.near(0), r)
        rows = pl.ds(t * 8, 8)
        for i in range(n):
            for x in range(box.sx):
                result[i, x, rows, :] = sums[i][x] * known["icount"][x, pl.ds(r, 8), :]
        pltpu.make_async_copy(result.at[:, :, rows], merged.at[pl.ds(group[0], n), :, rows], done).start()
        return 0

    lax.fori_loop(0, box.sy // 8, last, 0)
    copy.wait()


def merge(box, group, fields, edges, known, merged):
    p, k, r, n = box.planes, box.tiles, box.rows, len(group)
    f32 = jnp.float32
    sizes = fields[0].shape[1:]
    aliased = merged is not None
    operands = [*fields, *edges, *known]
    specs = [VMEM] * len(operands)
    return pl.pallas_call(
        functools.partial(fields_kernel, box, group, aliased),
        out_shape=jax.ShapeDtypeStruct((box.count, *sizes), f32),
        in_specs=specs + [ANY] * aliased,
        out_specs=ANY,
        scratch_shapes=[
            pltpu.VMEM((n, 3, p, r, LANES), f32),
            pltpu.VMEM((n, 9, k, r, LANES), f32),
            pltpu.VMEM((n, 3, p, r, LANES), f32),
            pltpu.VMEM((n, 9, k, r, LANES), f32),
            pltpu.VMEM((2, box.blocks, r, LANES), f32),
            pltpu.VMEM((n, *sizes), f32),
            pltpu.SemaphoreType.DMA(()),
        ],
        input_output_aliases={len(operands): 0} if aliased else {},
        compiler_params=params(14),
        name="merge",
    )(*operands, *([merged] if aliased else []))


def body(fields, volume_code, cut_flag, member_bits):
    count, sx, sy, _ = fields.shape
    size = lax.axis_size("gx")

    def from_x(value):
        if size == 1:
            return []
        if size == 2:
            return [lax.ppermute(value, "gx", ring("gx", 1))]
        return [lax.ppermute(value, "gx", ring("gx", -1)), lax.ppermute(value, "gx", ring("gx", 1))]

    groups = [list(range(count))[i : i + 2] for i in range(0, count, 2)]
    pairs, ints, zlo, zhi, ylo, yhi = pack(groups, fields, volume_code, cut_flag, member_bits)
    all_ints = [ints] + from_x(ints)
    low = lax.ppermute(zhi, "gz", ring("gz", 1))
    high = lax.ppermute(zlo, "gz", ring("gz", -1))
    box = Box(count, sx, sy, len(all_ints))
    shared = [[pairs[0]] + from_x(pairs[0])]
    ylo, yhi = add_corners(low, high, ylo, yhi)
    before = lax.ppermute(yhi, "gy", ring("gy", 1))
    after = lax.ppermute(ylo, "gy", ring("gy", -1))
    edge = join(low, high, before, after)
    all_edges = [edge] + from_x(edge)
    for pair in pairs[1:]:
        shared.append([pair] + from_x(pair))
    known = geometry(box, all_ints, all_edges)
    merged = None
    for group, blocks in zip(groups, shared):
        merged = merge(box, group, blocks, all_edges, known, merged)
    return merged


def solution(mesh):
    in_specs = (
        P(None, "gx", "gy", "gz"),
        P("gx", "gy", "gz"),
        P("gx", "gy", "gz"),
        P("gx", "gy", "gz"),
    )
    out_specs = P(None, "gx", "gy", "gz")
    return jax.shard_map(body, mesh=mesh, in_specs=in_specs, out_specs=out_specs, check_vma=False)
```

time: 151 us -> 60.8 us (0.40)
  other arithmetic: 41.1 us -> 0 us
  waiting for transfers between devices: 52.8 us -> 14.7 us
  Pallas kernels: 0 us -> 33.9 us
  local copies, waits for them, and re-layouts: 31.1 us -> 0 us
  starting transfers between devices: 24.1 us -> 11.9 us
    ppermute x24 -> x8, waiting for transfers between devices: 52.8 us -> 14.7 us  [the longest x4 12.1 us: from_x(): return [lax.ppermute(value, 'gx', ring('gx', 1))]]
    pallas_call x0 -> x6, Pallas kernels: none -> 33.9 us  [the longest x2 24.8 us: merge(): pl.pallas_call(functools.partial(fields_kernel, box, group, aliased), out...]
    concatenate x18 -> x0, other arithmetic: 19.2 us -> none  [the longest x16 19.1 us: extended(): block = jnp.concatenate([low, block, high], axis=dim)]
    ppermute x16 -> x0, local copies, waits for them, and re-layouts: 13.9 us -> none  [the longest x8 7.63 us: extended(): lax.ppermute(lax.slice_in_dim(block, 0, width, axis=dim), axis, backward)]
    slice x22 -> x0, local copies, waits for them, and re-layouts: 12.2 us -> none  [the longest x8 9.39 us: extended(): lax.slice_in_dim(block, 0, width, axis=dim)]
    ppermute x24 -> x8, starting transfers between devices: 24.1 us -> 11.9 us  [the longest x4 5.49 us: from_x(): return [lax.ppermute(value, 'gx', ring('gx', 1))]]
    mul x11 -> x0, other arithmetic: 7.17 us -> none  [the longest x9 4.53 us: pulled_sums(): sums = sums + member[None] * piece[:5]]
    add x3 -> x0, other arithmetic: 6.96 us -> none  [the longest x2 5.84 us: pulled_sums(): sums = sums + member[None] * piece[:5]]
  transfers between devices with their start and end apart: 24 -> 8, of which waited for: 18 -> 2; matrix products, arithmetic and copies ran while one was open for 9% -> 0% of each run, Pallas kernels for 0% -> 33%
where the time goes in v3:
time: 60.8 us; the launch traced here: 60.6 us
  Pallas kernels  33.9 us (56%)
  waiting for transfers between devices  14.7 us (24%)
  starting transfers between devices  11.9 us (20%)
    pallas_call x2, Pallas kernels, merge(): pl.pallas_call(functools.partial(fields_kernel, box, group, aliased), out...  24.8 us
    ppermute x4, waiting for transfers between devices, from_x(): return [lax.ppermute(value, 'gx', ring('gx', 1))]  12.1 us
    pallas_call x1, Pallas kernels, geometry(): pl.pallas_call(functools.partial(geometry_kernel, box), out_shape=geometr...  7.33 us
    ppermute x4, starting transfers between devices, from_x(): return [lax.ppermute(value, 'gx', ring('gx', 1))]  5.49 us
    ppermute x1, waiting for transfers between devices, body(): before = lax.ppermute(yhi, 'gy', ring('gy', 1))  2.65 us
    ppermute x1, starting transfers between devices, body(): after = lax.ppermute(ylo, 'gy', ring('gy', -1))  2.25 us
    ppermute x1, starting transfers between devices, body(): high = lax.ppermute(zlo, 'gz', ring('gz', -1))  2.01 us
    pallas_call x1, Pallas kernels, pack(): pl.pallas_call(pack_kernel, out_shape=(*pairs, pltpu.VMEM((2, sx, sy, sz)...  1.83 us
  transfers between devices with their start and end apart: 8, of which 2 were waited for; matrix products, arithmetic and copies ran while one was open for 0% of the time, Pallas kernels for 33%

profile of v3, /device:TPU:0, one launch (start us, length us, event | category | flops | bytes accessed | tf_op | source)
XLA Modules:
  0.0 60.6 jit_solution(12385483717122649558)
XLA Ops:
  0.0 1.8 %pack.1 = (f32[2,4,64,128]{3,2,1,0:T(8,128)S(1)}, f32[2,4,64,128]{3,2,1,0:T(8,128)S(1)}, s32[2,4,64,128]{3,2,1,0:T(8,128)S(1)}, f32[64,128]{1,0:T(8,128)S(1)}, f...) custom-call(f32[4,4,64,128]{3,2,1,0:T(8,128)} %fields.1, s32[4,64,128]{2,1,0:T(8,128)} %code.1, ...), custom_call_target="tpu_custom_call" | custom-call | tf_op jit(solution)/shard_map/pack/pallas_call | solution.py:101
  1.8 0.5 collective-permute-start.1
  2.4 2.0 %collective-permute-start.2 = (f32[64,128]{1,0:T(8,128)S(1)}, f32[64,128]{1,0:T(8,128)S(1)}, u32[]{:S(2)}, u32[]{:S(2)}) collective-permute-start(f32[64,128]{1,0:T(8,128)S(1)} %get-tuple-element.27), channel_id=1, source_target_pairs={{0,3},{1,0},{2,1},{3,2},{4,7},{5,4},{6,5},{7,6},{8,11},{9,8},{10,9... | collective-permute-start | bytes 98312 | tf_op jit(solution)/shard_map/ppermute | solution.py:548
  4.4 2.2 %collective-permute-start.6 = (s32[2,4,64,128]{3,2,1,0:T(8,128)S(1)}, s32[2,4,64,128]{3,2,1,0:T(8,128)S(1)}, u32[]{:S(2)}, u32[]{:S(2)}) collective-permute-start(s32[2,4,64,128]{3,2,1,0:T(8,128)S(1)} %get-tuple-element.32.refs_0_), channel_id=1, source_target_pairs={{0,16},{16,0},{1,17},{17,1},{2,18},{18,2},{3,19},{19,3},{4,20},{20... | collective-permute-start | bytes 786440 | tf_op jit(solution)/shard_map/ppermute | solution.py:541
  6.6 0.0 collective-permute-start.7
  6.6 2.0 %collective-permute-start = (f32[2,4,64,128]{3,2,1,0:T(8,128)S(1)}, f32[2,4,64,128]{3,2,1,0:T(8,128)S(1)}, u32[]{:S(2)}, u32[]{:S(2)}) collective-permute-start(f32[2,4,64,128]{3,2,1,0:T(8,128)S(1)} %get-tuple-element.25.refs_0_), channel_id=1, source_target_pairs={{0,16},{16,0},{1,17},{17,1},{2,18},{18,2},{3,19},{19,3},{4,20},{20... | collective-permute-start | bytes 786440 | tf_op jit(solution)/shard_map/ppermute | solution.py:541
  8.6 0.0 collective-permute-done.1.low.refs_0_
  8.6 0.0 collective-permute-done.2.high.refs_1_
  8.6 1.6 %collective-permute-start.3 = (f32[120,128]{1,0:T(8,128)S(1)}, f32[120,128]{1,0:T(8,128)S(1)}, u32[]{:S(2)}, u32[]{:S(2)}) collective-permute-start(f32[120,128]{1,0:T(8,128)S(1)} %get-tuple-element.30), channel_id=1, source_target_pairs={{0,4},{4,8},{8,12},{12,0},{1,5},{5,9},{9,13},{13,1},{2,6},{6,10},{... | collective-permute-start | bytes 184328 | tf_op jit(solution)/shard_map/ppermute | solution.py:552
  10.3 2.2 %collective-permute-start.4 = (f32[120,128]{1,0:T(8,128)S(1)}, f32[120,128]{1,0:T(8,128)S(1)}, u32[]{:S(2)}, u32[]{:S(2)}) collective-permute-start(f32[120,128]{1,0:T(8,128)S(1)} %get-tuple-element.31), channel_id=1, source_target_pairs={{0,12},{4,0},{8,4},{12,8},{1,13},{5,1},{9,5},{13,9},{2,14},{6,2},{... | collective-permute-start | bytes 184328 | tf_op jit(solution)/shard_map/ppermute | solution.py:553
  12.5 2.6 %collective-permute-done.3.refs_2_ = f32[120,128]{1,0:T(8,128)S(1)} collective-permute-done((f32[120,128]{1,0:T(8,128)S(1)}, f32[120,128]{1,0:T(8,128)S(1)}, u32[]{:S(2)}, u32[]{:S(2)}) %collective-permute-start.3) | collective-permute-done | bytes 61472 | tf_op jit(solution)/shard_map/ppermute | solution.py:552
  15.2 0.0 collective-permute-done.4.refs_3_
  15.2 1.3 %collective-permute-start.5 = (f32[368,128]{1,0:T(8,128)S(1)}, f32[368,128]{1,0:T(8,128)S(1)}, u32[]{:S(2)}, u32[]{:S(2)}) collective-permute-start(f32[368,128]{1,0:T(8,128)S(1)} %join.1.refs_2_), channel_id=1, source_target_pairs={{0,16},{16,0},{1,17},{17,1},{2,18},{18,2},{3,19},{19,3},{4,20},{20... | collective-permute-start | bytes 565256 | tf_op jit(solution)/shard_map/ppermute | solution.py:541
  16.4 0.0 collective-permute-done.6.refs_1_
  16.4 12.0 %collective-permute-done.5.refs_3_ = f32[368,128]{1,0:T(8,128)S(1)} collective-permute-done((f32[368,128]{1,0:T(8,128)S(1)}, f32[368,128]{1,0:T(8,128)S(1)}, u32[]{:S(2)}, u32[]{:S(2)}) %collective-permute-start.5) | collective-permute-done | bytes 188448 | tf_op jit(solution)/shard_map/ppermute | solution.py:541
  28.5 7.3 %geometry.1 = (f32[26,8,88,128]{3,2,1,0:T(8,128)S(1)}, f32[26,1,88,128]{3,2,1,0:T(8,128)S(1)}, f32[26,8,88,128]{3,2,1,0:T(8,128)S(1)}, f32[26,1,88,128]{3,2,1,0:...) custom-call(s32[2,4,64,128]{3,2,1,0:T(8,128)S(1)} %get-tuple-element, ...), custom_call_target="tpu_custom_call" | custom-call | tf_op jit(solution)/shard_map/geometry/pallas_call | solution.py:433
  35.8 0.0 collective-permute-done.7.refs_1_
  35.8 12.4 %merge.2.refs_15_ = f32[4,4,64,128]{3,2,1,0:T(8,128)} custom-call(f32[2,4,64,128]{3,2,1,0:T(8,128)S(1)} %get-tuple-element.44.refs_0_, f32[2,4,64,128]{3,2,1,0:T(8,128)S(1)} %collective-permute-done.7.refs_1_, f32[368,128]{1,0:T(8,128)S(1)} %join.1.refs_2_, f32[368,128]{1,0:T(8,128)S(1)} %collective-permute-done.5.refs_3_, ...), custom_call_target="tpu_custom_call" | custom-call | tf_op jit(solution)/shard_map/merge/pallas_call | solution.py:513
  48.2 0.0 collective-permute-done.refs_1_
  48.2 12.4 %merge.3 = f32[4,4,64,128]{3,2,1,0:T(8,128)} custom-call(f32[2,4,64,128]{3,2,1,0:T(8,128)S(1)} %get-tuple-element.25.refs_0_, f32[2,4,64,128]{3,2,1,0:T(8,128)S(1)} %collective-permute-done.refs_1_, f32[368,128]{1,0:T(8,128)S(1)} %join.1.refs_2_, f32[368,128]{1,0:T(8,128)S(1)} %collective-permute-done.5.refs_3_, ...), custom_call_target="tpu_custom_call", output_to_operand_aliasing={{}: (15, {})} | custom-call | tf_op jit(solution)/shard_map/merge/pallas_call | solution.py:513
  (2 shorter events, 0.0 us)
Async XLA Ops:
  1.8 6.8 %collective-permute-start.1 = (f32[64,128]{1,0:T(8,128)S(1)}, f32[64,128]{1,0:T(8,128)S(1)}, u32[]{:S(2)}, u32[]{:S(2)}) collective-permute-start(f32[64,128]{1,0:T(8,128)S(1)} %get-tuple-element.26), channel_id=1, source_target_pairs={{0,1},{1,2},{2,3},{3,0},{4,5},{5,6},{6,7},{7,4},{8,9},{9,10},{10,1... | collective-permute-start | bytes 98312 | tf_op jit(solution)/shard_map/ppermute | solution.py:547
  2.4 6.3 %collective-permute-start.2 = (f32[64,128]{1,0:T(8,128)S(1)}, f32[64,128]{1,0:T(8,128)S(1)}, u32[]{:S(2)}, u32[]{:S(2)}) collective-permute-start(f32[64,128]{1,0:T(8,128)S(1)} %get-tuple-element.27), channel_id=1, source_target_pairs={{0,3},{1,0},{2,1},{3,2},{4,7},{5,4},{6,5},{7,6},{8,11},{9,8},{10,9... | collective-permute-start | bytes 98312 | tf_op jit(solution)/shard_map/ppermute | solution.py:548
  4.4 12.1 %collective-permute-start.6 = (s32[2,4,64,128]{3,2,1,0:T(8,128)S(1)}, s32[2,4,64,128]{3,2,1,0:T(8,128)S(1)}, u32[]{:S(2)}, u32[]{:S(2)}) collective-permute-start(s32[2,4,64,128]{3,2,1,0:T(8,128)S(1)} %get-tuple-element.32.refs_0_), channel_id=1, source_target_pairs={{0,16},{16,0},{1,17},{17,1},{2,18},{18,2},{3,19},{19,3},{4,20},{20... | collective-permute-start | bytes 786440 | tf_op jit(solution)/shard_map/ppermute | solution.py:541
  6.6 29.2 %collective-permute-start.7 = (f32[2,4,64,128]{3,2,1,0:T(8,128)S(1)}, f32[2,4,64,128]{3,2,1,0:T(8,128)S(1)}, u32[]{:S(2)}, u32[]{:S(2)}) collective-permute-start(f32[2,4,64,128]{3,2,1,0:T(8,128)S(1)} %get-tuple-element.44.refs_0_), channel_id=1, source_target_pairs={{0,16},{16,0},{1,17},{17,1},{2,18},{18,2},{3,19},{19,3},{4,20},{20... | collective-permute-start | bytes 786440 | tf_op jit(solution)/shard_map/ppermute | solution.py:541
  6.6 41.6 %collective-permute-start = (f32[2,4,64,128]{3,2,1,0:T(8,128)S(1)}, f32[2,4,64,128]{3,2,1,0:T(8,128)S(1)}, u32[]{:S(2)}, u32[]{:S(2)}) collective-permute-start(f32[2,4,64,128]{3,2,1,0:T(8,128)S(1)} %get-tuple-element.25.refs_0_), channel_id=1, source_target_pairs={{0,16},{16,0},{1,17},{17,1},{2,18},{18,2},{3,19},{19,3},{4,20},{20... | collective-permute-start | bytes 786440 | tf_op jit(solution)/shard_map/ppermute | solution.py:541
  8.6 6.5 %collective-permute-start.3 = (f32[120,128]{1,0:T(8,128)S(1)}, f32[120,128]{1,0:T(8,128)S(1)}, u32[]{:S(2)}, u32[]{:S(2)}) collective-permute-start(f32[120,128]{1,0:T(8,128)S(1)} %get-tuple-element.30), channel_id=1, source_target_pairs={{0,4},{4,8},{8,12},{12,0},{1,5},{5,9},{9,13},{13,1},{2,6},{6,10},{... | collective-permute-start | bytes 184328 | tf_op jit(solution)/shard_map/ppermute | solution.py:552
  10.3 4.9 %collective-permute-start.4 = (f32[120,128]{1,0:T(8,128)S(1)}, f32[120,128]{1,0:T(8,128)S(1)}, u32[]{:S(2)}, u32[]{:S(2)}) collective-permute-start(f32[120,128]{1,0:T(8,128)S(1)} %get-tuple-element.31), channel_id=1, source_target_pairs={{0,12},{4,0},{8,4},{12,8},{1,13},{5,1},{9,5},{13,9},{2,14},{6,2},{... | collective-permute-start | bytes 184328 | tf_op jit(solution)/shard_map/ppermute | solution.py:553
  15.2 13.3 %collective-permute-start.5 = (f32[368,128]{1,0:T(8,128)S(1)}, f32[368,128]{1,0:T(8,128)S(1)}, u32[]{:S(2)}, u32[]{:S(2)}) collective-permute-start(f32[368,128]{1,0:T(8,128)S(1)} %join.1.refs_2_), channel_id=1, source_target_pairs={{0,16},{16,0},{1,17},{17,1},{2,18},{18,2},{3,19},{19,3},{4,20},{20... | collective-permute-start | bytes 565256 | tf_op jit(solution)/shard_map/ppermute | solution.py:541
